TPU v7x, 128 devices: a whole 4x4x4 slice. The times are simulated.
128 devices in a mesh: rep: 2 (over core), dp: 64 (over x, y, z).
Axes of the slice: x: 4, y: 4, z: 4, core: 2. Of those that a mesh axis runs over, the one named last changes fastest.
Arguments:
- g_w_gate: bfloat16 [128, 2, 640, 2048], P(('rep', 'dp')), parts along dimension 0
- g_w_up: bfloat16 [128, 2, 640, 2048], P(('rep', 'dp')), parts along dimension 0
- g_w_down: bfloat16 [128, 2, 2048, 640], P(('rep', 'dp')), parts along dimension 0
- w_gate: bfloat16 [2, 640, 2048], replicated
- w_up: bfloat16 [2, 640, 2048], replicated
- w_down: bfloat16 [2, 2048, 640], replicated
- m_w_gate: float32 [2, 640, 2048], P(None, 'dp')
- m_w_up: float32 [2, 640, 2048], P(None, 'dp')
- m_w_down: float32 [2, 2048, 640], P(None, 'dp')
- v_w_gate: float32 [2, 640, 2048], P(None, 'dp')
- v_w_up: float32 [2, 640, 2048], P(None, 'dp')
- v_w_down: float32 [2, 2048, 640], P(None, 'dp')
Outputs:
- output 1: bfloat16 [4, 640, 2048], P('rep'), parts along dimension 0
- output 2: bfloat16 [4, 640, 2048], P('rep'), parts along dimension 0
- output 3: bfloat16 [4, 2048, 640], P('rep'), parts along dimension 0
- output 4: float32 [4, 640, 2048], P('rep', 'dp'), parts along dimension 0
- output 5: float32 [4, 640, 2048], P('rep', 'dp'), parts along dimension 0
- output 6: float32 [4, 2048, 640], P('rep', 'dp'), parts along dimension 0
- output 7: float32 [4, 640, 2048], P('rep', 'dp'), parts along dimension 0
- output 8: float32 [4, 640, 2048], P('rep', 'dp'), parts along dimension 0
- output 9: float32 [4, 2048, 640], P('rep', 'dp'), parts along dimension 0
There are 2 independent parts. A program takes and returns all parts, laid end to end along the dimension named above; an argument that names none is the same for every part.
All inputs are finite; a program needn't handle non-finite values.
Results may differ from a plain program's by a relative error of at most 0.022.
Values are sent between devices in bfloat16 or wider.
A program may use at most 1.5 GiB of HBM per device.

v0:
```python
import jax
import jax.numpy as jnp
from jax import lax
from jax.sharding import PartitionSpec as P


def adamw(w, m, v, g):
    m = 0.9 * m + 0.1 * g
    v = 0.95 * v + 0.05 * g * g
    step = m * lax.rsqrt(v + 1e-8) + 0.1 * w
    return (w - 0.02 * step).astype(jnp.bfloat16), m, v


def solution(mesh):
    def step(*arrays):
        terms, weights, m, v = (arrays[i : i + 3] for i in (0, 3, 6, 9))
        gradients = [lax.psum_scatter(t[0], "dp", scatter_dimension=1, tiled=True).astype(jnp.float32) for t in terms]
        me = lax.axis_index("dp")
        own = [lax.dynamic_slice_in_dim(w, me * one.shape[1], one.shape[1], 1).astype(jnp.float32) for w, one in zip(weights, m, strict=True)]
        new = [adamw(w, m, v, g) for w, m, v, g in zip(own, m, v, gradients, strict=True)]
        whole = [lax.all_gather(one[0], "dp", axis=1, tiled=True) for one in new]
        return (*whole, *(one[1] for one in new), *(one[2] for one in new))

    all_of, cut = P(None, None, None), P(None, "dp", None)
    return jax.shard_map(
        step,
        mesh=mesh,
        in_specs=(P(("rep", "dp"), None, None, None),) * 3 + (all_of,) * 3 + (cut,) * 6,
        out_specs=(P("rep", None, None),) * 3 + (P("rep", "dp", None),) * 6,
        check_vma=False,
    )
```

profile of v0, /device:TPU:0, one launch (start us, length us, event | category | flops | bytes accessed | tf_op | source)
XLA Modules:
  0.0 792.5 jit_solution(10774733937931983659)
XLA Ops:
  7.2 0.0 all-reduce.5.cloned.1.call-start
  7.2 20.0 %copy_bitcast_fusion = (bf16[2,640,2048]{2,0,1:T(2,128)(2,1)}, bf16[2,640,2048]{2,0,1:T(2,128)(2,1)}) fusion(bf16[1,2,640,2048]{3,2,1,0:T(8,128)(2,1)} %param.13, bf16[1,2,640,2048]{3,2,1,0:T(8,128)(2,1)} %param.12), kind=kLoop, calls=%fused_computation | loop fusion | bytes 20971520 | tf_op jit(solution)/shard_map/squeeze | solution.py:17
  27.3 0.0 all-reduce.5.cloned.1.call-update
  27.3 0.0 copy-start.6
  27.3 0.0 copy-start
  27.3 0.0 copy-start.1
  27.3 0.0 copy-start.2
  27.3 0.0 copy-start.3
  27.3 0.0 copy-start.4
  27.4 0.0 copy-start.5
  27.4 0.0 reduce-scatter.2.cloned.1.call-start
  27.4 0.7 reduce-scatter.2.cloned.1.call-update
  28.1 0.0 all-gather.6.cloned.1.call-start
  28.2 0.0 copy-done.6
  28.2 0.6 dynamic-slice
  29.4 1.1 constant_dynamic-slice_fusion
  30.5 175.9 %all-reduce.5.cloned.1.call-done = (bf16[2,640,2048]{2,0,1:T(2,128)(2,1)}, bf16[2,640,2048]{2,0,1:T(2,128)(2,1)}) async-done(((bf16[2,640,2048]{2,0,1:T(2,128)(2,1)}, bf16[2,640,2048]{2,0,1:T(2,128)(2,1)}), (bf16[2,640,2048]{2,0,1:T(2,128)(2,1)}, bf16[2,640,2048]{2,0,1:T(2,128)(2,1)})) %all-reduce.5.cloned.1.call-update) | async-done | bytes 10485776
  206.4 0.0 copy-done
  206.4 0.0 copy-done.1
  206.4 2.0 fusion.14
  208.4 0.0 all-gather.6.cloned.1.call-update
  208.5 0.0 all-gather.4.cloned.1.call-start
  208.5 0.0 copy-done.2
  208.5 0.0 copy-done.3
  208.5 2.1 fusion.13
  210.6 0.0 all-gather.4.cloned.1.call-update
  210.6 0.0 all-gather.8.cloned.1.call-start
  210.7 359.7 %reduce-scatter.2.cloned.1.call-done = bf16[2,32,640]{2,1,0:T(8,128)(2,1)} async-done(((bf16[2,2048,640]{2,1,0:T(8,128)(2,1)}), bf16[2,32,640]{2,1,0:T(8,128)(2,1)}) %reduce-scatter.2.cloned.1.call-update) | async-done | bytes 81936 | tf_op jit(solution)/shard_map/reduce_scatter | solution.py:17
  570.3 0.0 copy-done.4
  570.3 0.0 copy-done.5
  570.3 1.7 fusion.8
  572.0 0.0 all-gather.8.cloned.1.call-update
  572.0 66.4 %all-gather.6.cloned.1.call-done = bf16[2,640,2048]{2,0,1:T(2,128)(2,1)} async-done(((bf16[2,10,2048]{2,0,1:T(2,128)(2,1)}), bf16[2,640,2048]{2,0,1:T(2,128)(2,1)}) %all-gather.6.cloned.1.call-update) | async-done | bytes 5242896 | tf_op jit(solution)/shard_map/all_gather | solution.py:21
  638.4 7.2 copy.32
  645.6 64.0 %all-gather.4.cloned.1.call-done = bf16[2,640,2048]{2,0,1:T(2,128)(2,1)} async-done(((bf16[2,10,2048]{2,0,1:T(2,128)(2,1)}), bf16[2,640,2048]{2,0,1:T(2,128)(2,1)}) %all-gather.4.cloned.1.call-update) | async-done | bytes 5242896 | tf_op jit(solution)/shard_map/all_gather | solution.py:21
  709.6 7.2 copy.31
  716.9 63.8 %all-gather.8.cloned.1.call-done = bf16[2,2048,640]{2,1,0:T(8,128)(2,1)} async-done(((bf16[2,32,640]{2,1,0:T(8,128)(2,1)}), bf16[2,2048,640]{2,1,0:T(8,128)(2,1)}) %all-gather.8.cloned.1.call-update) | async-done | bytes 5242896 | tf_op jit(solution)/shard_map/all_gather | solution.py:21
  780.7 5.3 copy.42
Async XLA Ops:
  7.2 199.2 %all-reduce.5.cloned.1.call-start = ((), (), s32[]{:S(2)}) async-start(), calls=%async_computation.5 | async-start | bytes 20971520
  27.3 0.9 copy-start.6
  27.3 179.1 %copy-start = (f32[2,10,2048]{2,0,1:T(2,128)S(1)}, f32[2,10,2048]{2,0,1:T(2,128)}, u32[]{:S(2)}) copy-start(f32[2,10,2048]{2,0,1:T(2,128)} %param.22) | copy-start | bytes 491524
  27.3 179.1 %copy-start.1 = (f32[2,10,2048]{2,0,1:T(2,128)S(1)}, f32[2,10,2048]{2,0,1:T(2,128)}, u32[]{:S(2)}) copy-start(f32[2,10,2048]{2,0,1:T(2,128)} %param.19) | copy-start | bytes 491524
  27.3 181.2 %copy-start.2 = (f32[2,10,2048]{2,0,1:T(2,128)S(1)}, f32[2,10,2048]{2,0,1:T(2,128)}, u32[]{:S(2)}) copy-start(f32[2,10,2048]{2,0,1:T(2,128)} %param.21) | copy-start | bytes 491524
  27.3 181.2 %copy-start.3 = (f32[2,10,2048]{2,0,1:T(2,128)S(1)}, f32[2,10,2048]{2,0,1:T(2,128)}, u32[]{:S(2)}) copy-start(f32[2,10,2048]{2,0,1:T(2,128)} %param.18) | copy-start | bytes 491524
  27.3 543.0 %copy-start.4 = (f32[2,32,640]{2,1,0:T(8,128)S(1)}, f32[2,32,640]{2,1,0:T(8,128)}, u32[]{:S(2)}) copy-start(f32[2,32,640]{2,1,0:T(8,128)} %param.23) | copy-start | bytes 491524
  27.4 543.0 %copy-start.5 = (f32[2,32,640]{2,1,0:T(8,128)S(1)}, f32[2,32,640]{2,1,0:T(8,128)}, u32[]{:S(2)}) copy-start(f32[2,32,640]{2,1,0:T(8,128)} %param.20) | copy-start | bytes 491524
  27.4 543.0 %reduce-scatter.2.cloned.1.call-start = ((), (), s32[]{:S(2)}) async-start(), calls=%async_computation.3 | async-start | bytes 5324800 | tf_op jit(solution)/shard_map/reduce_scatter | solution.py:17
  28.1 610.3 %all-gather.6.cloned.1.call-start = ((), (), s32[]{:S(2)}) async-start(), calls=%async_computation.2 | async-start | bytes 5324800 | tf_op jit(solution)/shard_map/all_gather | solution.py:21
  208.5 501.2 %all-gather.4.cloned.1.call-start = ((), (), s32[]{:S(2)}) async-start(), calls=%async_computation.1 | async-start | bytes 5324800 | tf_op jit(solution)/shard_map/all_gather | solution.py:21
  210.6 570.1 %all-gather.8.cloned.1.call-start = ((), (), s32[]{:S(2)}) async-start(), calls=%async_computation.4 | async-start | bytes 5324800 | tf_op jit(solution)/shard_map/all_gather | solution.py:21
Sparse Core Ops, SparseCore 0:
  27.4 178.9 all-reduce.4
  208.8 361.5 reduce-scatter.1
  573.8 64.5 all-gather.5
  641.7 67.8 all-gather.3
  712.4 68.2 all-gather.7
where the time goes:
time: 793 us
  waiting for transfers between devices  730 us (92%)
  local copies, waits for them, and re-layouts  41.5 us (5%)
  between operations  14.5 us (2%)
    reduce_scatter x1, waiting for transfers between devices, step(): lax.psum_scatter(t[0], 'dp', scatter_dimension=1, tiled=True)  360 us
    all_gather x3, waiting for transfers between devices, step(): whole = [lax.all_gather(one[0], 'dp', axis=1, tiled=True) for one in new]  194 us
    unnamed x6, waiting for transfers between devices  177 us
    unnamed x18, local copies, waits for them, and re-layouts  20.4 us
    squeeze x1, local copies, waits for them, and re-layouts, step(): t[0]  20 us
  transfers between devices with their start and end apart: 5, of which 5 were waited for; matrix products, arithmetic and copies ran while one was open for 3% of the time, Pallas kernels for 0%

commit v1 on v0

v1 whole, which is shorter than its diff:
```python
import jax
import jax.numpy as jnp
from jax import lax
from jax.experimental import pallas as pl
from jax.experimental.pallas import tpu as pltpu
from jax.sharding import PartitionSpec as P

MESH = pl.DeviceIdType.MESH
F32, BF16 = jnp.float32, jnp.bfloat16
CHUNKS = 2
COLS = 2048 // CHUNKS
TILES = 4 // CHUNKS


class Piece:
    def __init__(self, weight, chunk):
        self.weight, self.chunk = weight, chunk
        if weight < 2:
            self.axes = ((0, 1, 2), (1, 0, 2))[weight]
            self.lead1, self.lead2, self.lead3 = (4, 5), (5,), (2,)
            self.cols = COLS
        else:
            self.axes = ((2, 0, 1), (2, 1, 0))[chunk % 2]
            self.lead1, self.lead2, self.lead3 = (4, 4, TILES), (4, TILES), (TILES,)
            self.cols = 640

    def shape(self, lead, *front):
        return (*front, *lead, 8, self.cols)

    def scratch(self):
        one, two, three = self.lead1, self.lead2, self.lead3
        shapes = [
            (self.shape(one, 2, 2), BF16),
            (self.shape(one, 3, 2), BF16),
            (self.shape(two, 2, 2), F32),
            (self.shape(two, 2, 2), BF16),
            (self.shape(two, 3, 2), BF16),
            (self.shape(two, 2), F32),
            (self.shape(two, 2), BF16),
            (self.shape(three, 3, 2), BF16),
        ]
        if self.weight < 2:
            shapes.append((self.shape(three, 4, 2), BF16))
        return shapes

    def columns(self):
        return pl.ds(self.chunk * COLS, COLS)

    def first(self, ref, layer, p):
        if self.weight == 0:
            return ref.at[layer, p, :, :, :, self.columns()]
        if self.weight == 1:
            return ref.at[layer, :, p, :, :, self.columns()]
        return ref.at[layer, :, :, p, pl.ds(self.chunk * TILES, TILES)]

    def second(self, block, p):
        if self.weight == 2 and self.axes[1] == 1:
            return block.at[:, p]
        return block.at[p]

    def third(self, block, p):
        return block.at[pl.ds(p, 2)] if self.weight < 2 else block.at[p]

    def out2(self, ref, layer, p, pos):
        if self.weight == 0:
            return ref.at[layer, pos[0], p, :, :, self.columns()]
        if self.weight == 1:
            return ref.at[layer, p, pos[1], :, :, self.columns()]
        rows = pl.ds(self.chunk * TILES, TILES)
        if self.axes[1] == 0:
            return ref.at[layer, p, :, pos[2], rows]
        return ref.at[layer, :, p, pos[2], rows]

    def out3(self, ref, layer, p, pos):
        rows = pl.ds(self.chunk * TILES, TILES)
        if self.axes[2] == 1:
            return ref.at[layer, pos[0], p, pos[2], rows]
        return ref.at[layer, p, pos[1], pos[2], rows]


PIECES = [Piece(w, c) for c in range(CHUNKS) for w in range(3)]
COPIES = 36 * len(PIECES)
LOADS = 4 * len(PIECES) + 9


def each_slab(lead, body):
    outer = 1
    for n in lead[:-1]:
        outer *= n

    def some(i):
        front = []
        for n in reversed(lead[:-1]):
            front.insert(0, lax.rem(i, n))
            i = lax.div(i, n)
        for j in range(lead[-1]):
            body((*front, j))

    if outer == 1:
        some(jnp.int32(0))
    else:
        lax.fori_loop(0, outer, lambda i, c: (some(i), c)[1], 0)


def add_into(lead, terms, outs):
    def body(index):
        total = terms[0][index].astype(F32)
        for t in terms[1:]:
            total = total + t[index].astype(F32)
        for o in outs:
            o[index] = total.astype(o.dtype)

    each_slab(lead, body)


def adamw(w, m, v, g):
    m = 0.9 * m + 0.1 * g
    v = 0.95 * v + 0.05 * g * g
    step = m * lax.rsqrt(v + 1e-8) + 0.1 * w
    return w - 0.02 * step, m, v


def kernel(*refs):
    refs = list(refs)

    def take(n):
        got, refs[:n] = refs[:n], []
        return got

    grads, weights, ms, vs = take(3), take(3), take(3), take(3)
    new_w, new_m, new_v = take(3), take(3), take(3)
    m_in, v_in, w_in = take(3), take(3), take(3)
    m_win, v_win = take(2), take(2)
    bufs = [take(len(p.scratch())) for p in PIECES]
    send_sem, recv_sem, load_sem = take(3)

    me = lax.axis_index("dp")
    pos = (lax.div(me, 16), lax.rem(lax.div(me, 4), 4), lax.rem(me, 4))
    stride = (16, 4, 1)

    def at(axis, d):
        return lax.rem(pos[axis] + d, 4)

    def neighbour(axis, d):
        return me + (at(axis, d) - pos[axis]) * stride[axis]

    plus = [neighbour(a, 1) for a in range(3)]
    minus = [neighbour(a, 3) for a in range(3)]

    barrier = pltpu.get_barrier_semaphore()
    for other in (*plus, *minus):
        pl.semaphore_signal(barrier, inc=1, device_id={"dp": other}, device_id_type=MESH)

    sent, loads = [], []

    def remote(src, dst, axis, forward):
        i = len(sent)
        copy = pltpu.make_async_remote_copy(
            src_ref=src,
            dst_ref=dst,
            send_sem=send_sem.at[i],
            recv_sem=recv_sem.at[i],
            device_id={"dp": (plus if forward else minus)[axis]},
            device_id_type=MESH,
        )
        sent.append(copy)
        copy.start()
        return copy

    def load(src, dst):
        copy = pltpu.make_async_copy(src, dst, load_sem.at[len(loads)])
        loads.append(copy)
        copy.start()
        return copy

    class Scatter:
        def __init__(self, axis, recv, far, near, lead, relay_term):
            self.axis, self.recv, self.far, self.near = axis, recv, far, near
            self.lead, self.relay_term = lead, relay_term
            self.got = {}

        def send_far(self):
            for layer in (0, 1):
                self.got["far", layer] = remote(self.far(layer), self.recv.at[0, layer], self.axis, layer == 0)

        def send_near(self):
            for layer in (1, 0):
                self.got["near", layer] = remote(self.near(layer), self.recv.at[1, layer], self.axis, layer == 1)

        def relay(self):
            for layer in (0, 1):
                self.got["far", layer].wait_recv()
                here = self.recv.at[0, layer]
                add_into(self.lead, (here, self.relay_term(layer)), (here,))
                self.got["relay", layer] = remote(here, self.recv.at[2, layer], self.axis, layer == 0)

        def wait(self, layer):
            self.got["near", layer].wait_recv()
            self.got["relay", layer].wait_recv()

    class Gather:
        def __init__(self, axis, block):
            self.axis, self.block = axis, block
            self.got = {}

        def send(self, layer, p, forward, key):
            ref = self.block(layer, p)
            self.got[key] = remote(ref, ref, self.axis, forward)

        def start(self):
            mine = pos[self.axis]
            self.send(0, mine, True, "from minus 0")
            self.send(1, mine, False, "from plus 1")
            self.send(1, mine, True, "from minus 1")
            self.send(0, mine, False, "from plus 0")

        def forward(self):
            self.got["from minus 0"].wait_recv()
            self.send(0, at(self.axis, 3), True, "far 0")
            self.got["from plus 1"].wait_recv()
            self.send(1, at(self.axis, 1), False, "far 1")

        def finish(self):
            for key in ("from minus 1", "from plus 0", "far 0", "far 1"):
                self.got[key].wait_recv()

    class Flow:
        def __init__(self, piece, buf):
            self.piece, self.buf = piece, buf
            a1, a2, a3 = piece.axes
            g = grads[piece.weight]
            own1, recv1, sum1, send1, recv2, sum2, send2, recv3 = buf[:8]
            self.scatter1 = Scatter(
                a1,
                recv1,
                lambda layer: piece.first(g, layer, at(a1, 2)),
                lambda layer: piece.first(g, layer, at(a1, 1 if layer else 3)),
                piece.lead1,
                lambda layer: own1.at[layer, 1],
            )
            self.scatter2 = Scatter(
                a2,
                recv2,
                lambda layer: send1.at[layer, 0],
                lambda layer: send1.at[layer, 1],
                piece.lead2,
                lambda layer: sum1.at[layer, 1],
            )
            self.scatter3 = Scatter(
                a3,
                recv3,
                lambda layer: piece.third(send2.at[layer], at(a3, 2)),
                lambda layer: piece.third(send2.at[layer], at(a3, 1 if layer else 3)),
                piece.lead3,
                lambda layer: piece.third(sum2.at[layer], at(a3, 3 if layer else 1)),
            )
            w = new_w[piece.weight]
            if piece.weight < 2:
                windows = buf[8]
                self.gather3 = Gather(a3, lambda layer, p: windows.at[p, layer])
            else:
                self.gather3 = Gather(a3, lambda layer, p: piece.out3(w, layer, p, pos))
            self.gather2 = Gather(a2, lambda layer, p: piece.out2(w, layer, p, pos))
            self.gather1 = Gather(a1, lambda layer, p: piece.first(w, layer, p))

        def load(self):
            piece, own1 = self.piece, self.buf[0]
            a1, g = piece.axes[0], grads[piece.weight]
            self.loaded = [[None, None], [None, None]]
            for which in (1, 0):
                for layer in (0, 1):
                    p = at(a1, (3 if layer else 1) if which else 0)
                    self.loaded[layer][which] = load(piece.first(g, layer, p), own1.at[layer, which])

        def far1(self):
            self.scatter1.send_far()

        def near1(self):
            self.scatter1.send_near()

        def relay1(self):
            for layer in (0, 1):
                self.loaded[layer][1].wait()
            self.scatter1.relay()

        def sum1(self):
            piece = self.piece
            own1, recv1, sum1, send1 = self.buf[:4]
            a2 = piece.axes[1]
            for layer in (0, 1):
                self.loaded[layer][0].wait()
                self.scatter1.wait(layer)

            def reduce(layer, d, out):
                p = at(a2, d)
                terms = (own1.at[layer, 0], recv1.at[1, layer], recv1.at[2, layer])
                add_into(piece.lead2, [piece.second(t, p) for t in terms], (out,))

            for layer in (0, 1):
                reduce(layer, 2, send1.at[layer, 0])
            self.scatter2.send_far()
            for layer in (1, 0):
                reduce(layer, 1 if layer else 3, send1.at[layer, 1])
            self.scatter2.send_near()
            for layer in (0, 1):
                reduce(layer, 3 if layer else 1, sum1.at[layer, 1])
            for layer in (0, 1):
                reduce(layer, 0, sum1.at[layer, 0])

        def relay2(self):
            self.scatter2.relay()

        def sum2(self):
            sum1, _, recv2, sum2, send2 = self.buf[2:7]
            for layer in (0, 1):
                self.scatter2.wait(layer)
                terms = (sum1.at[layer, 0], recv2.at[1, layer], recv2.at[2, layer])
                add_into(self.piece.lead2, terms, (sum2.at[layer], send2.at[layer]))
            self.scatter3.send_far()
            self.scatter3.send_near()

        def relay3(self):
            self.scatter3.relay()

        def step(self):
            piece = self.piece
            sum2, recv3 = self.buf[5], self.buf[7]
            a3, k = piece.axes[2], piece.weight
            for layer in (0, 1):
                self.scatter3.wait(layer)
                terms = (piece.third(sum2.at[layer], pos[a3]), recv3.at[1, layer], recv3.at[2, layer])
                for j in range(piece.lead3[0]):
                    g = terms[0][j] + terms[1][j].astype(F32) + terms[2][j].astype(F32)
                    g = g.astype(BF16).astype(F32)
                    if k < 2:
                        rows, cols = pl.ds(8 * j, 8), piece.columns()
                        w, m, v = adamw(
                            w_in[k][layer, j, :, cols].astype(F32), m_win[k][layer, rows, cols], v_win[k][layer, rows, cols], g
                        )
                        m_win[k][layer, rows, cols] = m
                        v_win[k][layer, rows, cols] = v
                        row = lax.broadcasted_iota(jnp.int32, w.shape, 0) + 8 * j
                        mine = (row >= 2 * pos[2]) & (row < 2 * pos[2] + 10)
                        self.buf[8][pos[2], layer, j] = jnp.where(mine, w, 0.0).astype(BF16)
                    else:
                        t = piece.chunk * TILES + j
                        w, m, v = adamw(w_in[k][layer, t].astype(F32), m_in[k][layer, t], v_in[k][layer, t], g)
                        new_m[k][layer, t] = m
                        new_v[k][layer, t] = v
                        new_w[k][layer, pos[0], pos[1], pos[2], t] = w.astype(BF16)
            self.gather3.start()

        def forward3(self):
            self.gather3.forward()

        def merge(self):
            piece = self.piece
            self.gather3.finish()
            if piece.weight < 2:
                windows, k = self.buf[8], piece.weight
                for layer in (0, 1):
                    for t in range(5):
                        parts = [windows[t - 1, layer, 1]] if t else []
                        parts += [windows[t, layer, 0]] if t < 4 else []
                        whole = parts[0] if len(parts) == 1 else (parts[0].astype(F32) + parts[1].astype(F32)).astype(BF16)
                        new_w[k][layer, pos[0], pos[1], t, :, piece.columns()] = whole
            self.gather2.start()

        def forward2(self):
            self.gather2.forward()

        def out1(self):
            self.gather2.finish()
            self.gather1.start()

        def forward1(self):
            self.gather1.forward()

        def done(self):
            self.gather1.finish()

    flows = [Flow(p, b) for p, b in zip(PIECES, bufs, strict=True)]
    groups = [flows[3 * c : 3 * c + 3] for c in range(CHUNKS)]

    for f in flows:
        f.load()
    state_loads = []
    for k in range(3):
        state_loads.append([load(ms[k], m_in[k]), load(vs[k], v_in[k])])
        own = weights[k].at[:, pos[0], pos[1], pl.ds(pos[2], 2)] if k < 2 else weights[k].at[:, pos[0], pos[1], pos[2]]
        state_loads[k].append(load(own, w_in[k]))
    pl.semaphore_wait(barrier, 6)

    def do(c, *names):
        for name in names:
            for f in groups[c]:
                getattr(f, name)()

    do(0, "far1", "near1")
    for k in range(3):
        for copy in state_loads[k]:
            copy.wait()
    for k in range(2):
        for win, data in ((m_win[k], m_in[k]), (v_win[k], v_in[k])):
            win[...] = jnp.zeros_like(win)
            for layer in (0, 1):
                for r in range(10):
                    win[layer, pl.ds(2 * pos[2] + r, 1), :] = data[r, pl.ds(layer, 1), :]
    do(0, "relay1")
    do(1, "far1")
    do(0, "sum1")
    do(1, "near1", "relay1")
    do(0, "relay2", "sum2", "relay3", "step", "forward3", "merge", "forward2")
    do(1, "sum1")
    do(0, "out1")
    do(1, "relay2", "sum2")
    do(0, "forward1")
    do(1, "relay3", "step", "forward3", "merge", "forward2", "out1", "forward1")

    for k in range(2):
        for win, out in ((m_win[k], new_m[k]), (v_win[k], new_v[k])):
            for layer in (0, 1):
                for r in range(10):
                    out[r, pl.ds(layer, 1), :] = win[layer, pl.ds(2 * pos[2] + r, 1), :]
    do(0, "done")
    do(1, "done")
    for copy in sent:
        copy.wait_send()


def solution(mesh):
    def step(*arrays):
        terms, weights, m, v = (arrays[i : i + 3] for i in (0, 3, 6, 9))
        shapes = ((2, 4, 4, 5, 8, 2048), (2, 4, 4, 5, 8, 2048), (2, 4, 4, 4, 4, 8, 640))
        terms = [t.reshape(s) for t, s in zip(terms, shapes, strict=True)]
        weights = [w.reshape(s) for w, s in zip(weights, shapes, strict=True)]

        def state_in(x):
            return x.transpose(1, 0, 2) if x.shape[1] == 10 else x.reshape(2, 4, 8, 640)

        m, v = [state_in(x) for x in m], [state_in(x) for x in v]
        state_shapes = [x.shape for x in m]
        outs = [(s, BF16) for s in shapes] + [(s, F32) for s in state_shapes] * 2
        scratch = [pltpu.VMEM(s, F32) for s in state_shapes] * 2
        scratch += [pltpu.VMEM((2, 2, 8, 2048), BF16)] * 2 + [pltpu.VMEM((2, 4, 8, 640), BF16)]
        scratch += [pltpu.VMEM((2, 16, 2048), F32)] * 4
        scratch += [pltpu.VMEM(s, d) for p in PIECES for s, d in p.scratch()]
        scratch += [pltpu.SemaphoreType.DMA((COPIES,)), pltpu.SemaphoreType.DMA((COPIES,)), pltpu.SemaphoreType.DMA((LOADS,))]
        new = pl.pallas_call(
            kernel,
            name="step",
            out_shape=[pltpu.VMEM(s, d) for s, d in outs],
            in_specs=[pl.BlockSpec(memory_space=pl.ANY)] * 12,
            out_specs=[pl.BlockSpec(memory_space=pltpu.VMEM)] * 9,
            scratch_shapes=scratch,
            compiler_params=pltpu.CompilerParams(collective_id=0, has_side_effects=True, vmem_limit_bytes=46 * 2**20),
        )(*terms, *weights, *m, *v)

        def state_out(x):
            return x.transpose(1, 0, 2) if x.shape[0] == 10 else x.reshape(2, 32, 640)

        whole = [w.reshape(s) for w, s in zip(new[:3], ((2, 640, 2048), (2, 640, 2048), (2, 2048, 640)), strict=True)]
        return (*whole, *(state_out(x) for x in new[3:]))

    all_of, cut = P(None, None, None), P(None, "dp", None)
    return jax.shard_map(
        step,
        mesh=mesh,
        in_specs=(P(("rep", "dp"), None, None, None),) * 3 + (all_of,) * 3 + (cut,) * 6,
        out_specs=(P("rep", None, None),) * 3 + (P("rep", "dp", None),) * 6,
        check_vma=False,
    )
```

time: 793 us -> 166 us (0.21)
  waiting for transfers between devices: 730 us -> 0 us
  Pallas kernels: 0 us -> 154 us
  local copies, waits for them, and re-layouts: 41.5 us -> 11.1 us
  between operations: 14.5 us -> 0.66 us
    reduce_scatter x1 -> x0, waiting for transfers between devices: 360 us -> none  [step(): lax.psum_scatter(t[0], 'dp', scatter_dimension=1, tiled=True)]
    all_gather x3 -> x0, waiting for transfers between devices: 194 us -> none  [step(): whole = [lax.all_gather(one[0], 'dp', axis=1, tiled=True) for one in new]]
    unnamed x6 -> x0, waiting for transfers between devices: 177 us -> none
    pallas_call x0 -> x1, Pallas kernels: none -> 154 us  [step(): pl.pallas_call(kernel, name='step', out_shape=[pltpu.VMEM(s, d) for s, d...]
    squeeze x1 -> x0, local copies, waits for them, and re-layouts: 20 us -> none  [step(): t[0]]
    unnamed x18 -> x9, local copies, waits for them, and re-layouts: 20.4 us -> 11.1 us
  transfers between devices with their start and end apart: 5 -> 0, of which waited for: 5 -> 0; matrix products, arithmetic and copies ran while one was open for 3% -> 0% of each run, Pallas kernels for 0% -> 0%
where the time goes in v1:
time: 166 us
  Pallas kernels  154 us (93%)
  local copies, waits for them, and re-layouts  11.1 us (7%)
    pallas_call x1, Pallas kernels, step(): pl.pallas_call(kernel, name='step', out_shape=[pltpu.VMEM(s, d) for s, d...  154 us
    unnamed x9, local copies, waits for them, and re-layouts  11.1 us

profile of v1, /device:TPU:0, one launch (start us, length us, event | category | flops | bytes accessed | tf_op | source)
XLA Modules:
  0.0 166.2 jit_solution(15630039905434112179)
XLA Ops:
  0.6 154.4 %step.1 = (bf16[2,4,4,5,8,2048]{5,4,3,2,1,0:T(8,128)(2,1)S(1)}, bf16[2,4,4,5,8,2048]{5,4,3,2,1,0:T(8,128)(2,1)S(1)}, bf16[2,4,4,4,4,8,640]{6,5,4,3,2,1,0:T(8,128...) custom-call(bf16[2,4,4,5,8,2048]{5,4,3,2,1,0:T(8,128)(2,1)} %bitcast, ...), custom_call_target="tpu_custom_call" | custom-call | tf_op jit(solution)/shard_map/step/pallas_call | solution.py:449
  155.1 2.4 %copy.30 = bf16[2,640,2048]{2,1,0:T(8,128)(2,1)} copy(bf16[2,640,2048]{2,1,0:T(8,128)(2,1)S(1)} %bitcast.23) | data formatting | bytes 10485760
  157.5 2.4 %copy.31 = bf16[2,640,2048]{2,1,0:T(8,128)(2,1)} copy(bf16[2,640,2048]{2,1,0:T(8,128)(2,1)S(1)} %bitcast.22) | data formatting | bytes 10485760
  159.8 0.7 copy.33
  160.5 0.7 copy.34
  161.1 0.7 copy.35
  161.8 0.7 copy.36
  162.5 0.7 copy.37
  163.1 0.7 copy.38
  163.8 2.4 %copy.32 = bf16[2,2048,640]{2,1,0:T(8,128)(2,1)} copy(bf16[2,2048,640]{2,1,0:T(8,128)(2,1)S(1)} %bitcast.21) | data formatting | bytes 10485760

commit v2 on v1

--- a/solution.py
+++ b/solution.py
@@ -5,9 +5,19 @@
 from jax.experimental.pallas import tpu as pltpu
 from jax.sharding import PartitionSpec as P
 
+STAGES = (
+    *("far1", "near1", "relay1", "sum1", "relay2", "sum2", "relay3", "step"),
+    *("forward3", "merge", "forward2", "out1", "rest1", "forward1"),
+)
+ORDER = (
+    "abcabcabcdefeabcfefddabcihfieadgibcehhfagdlcgeibalklehbafgdc"
+    "jihkfkgcjlebjaidhfebdhekdgchldjfgahbilgehdkjgcaifgdbljiefhjg"
+    "kcjkcicbbjaaklfhgijkfleefkjddilkihggiljhkljkljkl"
+)
+
 MESH = pl.DeviceIdType.MESH
 F32, BF16 = jnp.float32, jnp.bfloat16
-CHUNKS = 2
+CHUNKS = 4
 COLS = 2048 // CHUNKS
 TILES = 4 // CHUNKS
 
@@ -79,27 +89,8 @@
 
 
 PIECES = [Piece(w, c) for c in range(CHUNKS) for w in range(3)]
-COPIES = 36 * len(PIECES)
+COPIES = [12 * n for n in (3 * CHUNKS, 3 * CHUNKS, 2 * CHUNKS, CHUNKS)]
 LOADS = 4 * len(PIECES) + 9
-
-
-def each_slab(lead, body):
-    outer = 1
-    for n in lead[:-1]:
-        outer *= n
-
-    def some(i):
-        front = []
-        for n in reversed(lead[:-1]):
-            front.insert(0, lax.rem(i, n))
-            i = lax.div(i, n)
-        for j in range(lead[-1]):
-            body((*front, j))
-
-    if outer == 1:
-        some(jnp.int32(0))
-    else:
-        lax.fori_loop(0, outer, lambda i, c: (some(i), c)[1], 0)
 
 
 def add_into(lead, terms, outs):
@@ -110,7 +101,10 @@
         for o in outs:
             o[index] = total.astype(o.dtype)
 
-    each_slab(lead, body)
+    if len(lead) + (lead[-1] == 5) > 2:
+        lax.fori_loop(0, lead[0], lambda i, c: (body(i), c)[1], 0)
+    else:
+        body(...)
 
 
 def adamw(w, m, v, g):
@@ -132,7 +126,8 @@
     m_in, v_in, w_in = take(3), take(3), take(3)
     m_win, v_win = take(2), take(2)
     bufs = [take(len(p.scratch())) for p in PIECES]
-    send_sem, recv_sem, load_sem = take(3)
+    send_sems, recv_sems = take(4), take(4)
+    (load_sem,) = take(1)
 
     me = lax.axis_index("dp")
     pos = (lax.div(me, 16), lax.rem(lax.div(me, 4), 4), lax.rem(me, 4))
@@ -151,21 +146,37 @@
     for other in (*plus, *minus):
         pl.semaphore_signal(barrier, inc=1, device_id={"dp": other}, device_id_type=MESH)
 
-    sent, loads = [], []
-
-    def remote(src, dst, axis, forward):
-        i = len(sent)
+    sent, loads = [[], [], [], []], []
+
+    def remote(src, dst, axis, forward, kind):
+        i = len(sent[kind])
         copy = pltpu.make_async_remote_copy(
             src_ref=src,
             dst_ref=dst,
-            send_sem=send_sem.at[i],
-            recv_sem=recv_sem.at[i],
+            send_sem=send_sems[kind].at[i],
+            recv_sem=recv_sems[kind].at[i],
             device_id={"dp": (plus if forward else minus)[axis]},
             device_id_type=MESH,
         )
-        sent.append(copy)
+        sent[kind].append((src, dst))
         copy.start()
         return copy
+
+    def wait_sent(kind):
+        src, dst = sent[kind][0]
+
+        def one(i, c):
+            pltpu.make_async_remote_copy(
+                src_ref=src,
+                dst_ref=dst,
+                send_sem=send_sems[kind].at[i],
+                recv_sem=recv_sems[kind].at[i],
+                device_id={"dp": plus[0]},
+                device_id_type=MESH,
+            ).wait_send()
+            return c
+
+        lax.fori_loop(0, len(sent[kind]), one, 0)
 
     def load(src, dst):
         copy = pltpu.make_async_copy(src, dst, load_sem.at[len(loads)])
@@ -174,43 +185,46 @@
         return copy
 
     class Scatter:
-        def __init__(self, axis, recv, far, near, lead, relay_term):
-            self.axis, self.recv, self.far, self.near = axis, recv, far, near
+        def __init__(self, kind, axis, recv, far, near, lead, relay_term):
+            self.kind, self.axis, self.recv, self.far, self.near = kind, axis, recv, far, near
             self.lead, self.relay_term = lead, relay_term
             self.got = {}
 
         def send_far(self):
             for layer in (0, 1):
-                self.got["far", layer] = remote(self.far(layer), self.recv.at[0, layer], self.axis, layer == 0)
+                self.got["far", layer] = remote(self.far(layer), self.recv.at[0, layer], self.axis, layer == 0, self.kind)
 
         def send_near(self):
             for layer in (1, 0):
-                self.got["near", layer] = remote(self.near(layer), self.recv.at[1, layer], self.axis, layer == 1)
+                self.got["near", layer] = remote(self.near(layer), self.recv.at[1, layer], self.axis, layer == 1, self.kind)
 
         def relay(self):
             for layer in (0, 1):
                 self.got["far", layer].wait_recv()
                 here = self.recv.at[0, layer]
                 add_into(self.lead, (here, self.relay_term(layer)), (here,))
-                self.got["relay", layer] = remote(here, self.recv.at[2, layer], self.axis, layer == 0)
+                self.got["relay", layer] = remote(here, self.recv.at[2, layer], self.axis, layer == 0, self.kind)
 
         def wait(self, layer):
             self.got["near", layer].wait_recv()
             self.got["relay", layer].wait_recv()
 
     class Gather:
-        def __init__(self, axis, block):
-            self.axis, self.block = axis, block
+        def __init__(self, kind, axis, block):
+            self.kind, self.axis, self.block = kind, axis, block
             self.got = {}
 
         def send(self, layer, p, forward, key):
             ref = self.block(layer, p)
-            self.got[key] = remote(ref, ref, self.axis, forward)
+            self.got[key] = remote(ref, ref, self.axis, forward, self.kind)
 
         def start(self):
             mine = pos[self.axis]
             self.send(0, mine, True, "from minus 0")
             self.send(1, mine, False, "from plus 1")
+
+        def start_rest(self):
+            mine = pos[self.axis]
             self.send(1, mine, True, "from minus 1")
             self.send(0, mine, False, "from plus 0")
 
@@ -228,9 +242,11 @@
         def __init__(self, piece, buf):
             self.piece, self.buf = piece, buf
             a1, a2, a3 = piece.axes
+            last = 2 if piece.weight < 2 else 3
             g = grads[piece.weight]
             own1, recv1, sum1, send1, recv2, sum2, send2, recv3 = buf[:8]
             self.scatter1 = Scatter(
+                0,
                 a1,
                 recv1,
                 lambda layer: piece.first(g, layer, at(a1, 2)),
@@ -239,6 +255,7 @@
                 lambda layer: own1.at[layer, 1],
             )
             self.scatter2 = Scatter(
+                1,
                 a2,
                 recv2,
                 lambda layer: send1.at[layer, 0],
@@ -247,6 +264,7 @@
                 lambda layer: sum1.at[layer, 1],
             )
             self.scatter3 = Scatter(
+                last,
                 a3,
                 recv3,
                 lambda layer: piece.third(send2.at[layer], at(a3, 2)),
@@ -257,11 +275,11 @@
             w = new_w[piece.weight]
             if piece.weight < 2:
                 windows = buf[8]
-                self.gather3 = Gather(a3, lambda layer, p: windows.at[p, layer])
+                self.gather3 = Gather(last, a3, lambda layer, p: windows.at[p, layer])
             else:
-                self.gather3 = Gather(a3, lambda layer, p: piece.out3(w, layer, p, pos))
-            self.gather2 = Gather(a2, lambda layer, p: piece.out2(w, layer, p, pos))
-            self.gather1 = Gather(a1, lambda layer, p: piece.first(w, layer, p))
+                self.gather3 = Gather(last, a3, lambda layer, p: piece.out3(w, layer, p, pos))
+            self.gather2 = Gather(1, a2, lambda layer, p: piece.out2(w, layer, p, pos))
+            self.gather1 = Gather(0, a1, lambda layer, p: piece.first(w, layer, p))
 
         def load(self):
             piece, own1 = self.piece, self.buf[0]
@@ -329,26 +347,25 @@
             for layer in (0, 1):
                 self.scatter3.wait(layer)
                 terms = (piece.third(sum2.at[layer], pos[a3]), recv3.at[1, layer], recv3.at[2, layer])
-                for j in range(piece.lead3[0]):
-                    g = terms[0][j] + terms[1][j].astype(F32) + terms[2][j].astype(F32)
-                    g = g.astype(BF16).astype(F32)
-                    if k < 2:
-                        rows, cols = pl.ds(8 * j, 8), piece.columns()
-                        w, m, v = adamw(
-                            w_in[k][layer, j, :, cols].astype(F32), m_win[k][layer, rows, cols], v_win[k][layer, rows, cols], g
-                        )
-                        m_win[k][layer, rows, cols] = m
-                        v_win[k][layer, rows, cols] = v
-                        row = lax.broadcasted_iota(jnp.int32, w.shape, 0) + 8 * j
-                        mine = (row >= 2 * pos[2]) & (row < 2 * pos[2] + 10)
-                        self.buf[8][pos[2], layer, j] = jnp.where(mine, w, 0.0).astype(BF16)
-                    else:
-                        t = piece.chunk * TILES + j
-                        w, m, v = adamw(w_in[k][layer, t].astype(F32), m_in[k][layer, t], v_in[k][layer, t], g)
-                        new_m[k][layer, t] = m
-                        new_v[k][layer, t] = v
-                        new_w[k][layer, pos[0], pos[1], pos[2], t] = w.astype(BF16)
+                g = terms[0][...] + terms[1][...].astype(F32) + terms[2][...].astype(F32)
+                g = g.astype(BF16).astype(F32)
+                if k < 2:
+                    cols = piece.columns()
+                    w, m, v = w_in[k][layer, :, :, cols].astype(F32), m_win[k][layer, :, :, cols], v_win[k][layer, :, :, cols]
+                    w, m, v = adamw(w, m, v, g)
+                    m_win[k][layer, :, :, cols] = m
+                    v_win[k][layer, :, :, cols] = v
+                    row = lax.broadcasted_iota(jnp.int32, w.shape, 1) + 8 * lax.broadcasted_iota(jnp.int32, w.shape, 0)
+                    mine = (row >= 2 * pos[2]) & (row < 2 * pos[2] + 10)
+                    self.buf[8][pos[2], layer] = jnp.where(mine, w, 0.0).astype(BF16)
+                else:
+                    t = pl.ds(piece.chunk * TILES, TILES)
+                    w, m, v = adamw(w_in[k][layer, t].astype(F32), m_in[k][layer, t], v_in[k][layer, t], g)
+                    new_m[k][layer, t] = m
+                    new_v[k][layer, t] = v
+                    new_w[k][layer, pos[0], pos[1], pos[2], t] = w.astype(BF16)
             self.gather3.start()
+            self.gather3.start_rest()
 
         def forward3(self):
             self.gather3.forward()
@@ -359,12 +376,13 @@
             if piece.weight < 2:
                 windows, k = self.buf[8], piece.weight
                 for layer in (0, 1):
-                    for t in range(5):
-                        parts = [windows[t - 1, layer, 1]] if t else []
-                        parts += [windows[t, layer, 0]] if t < 4 else []
-                        whole = parts[0] if len(parts) == 1 else (parts[0].astype(F32) + parts[1].astype(F32)).astype(BF16)
-                        new_w[k][layer, pos[0], pos[1], t, :, piece.columns()] = whole
+                    out = new_w[k].at[layer, pos[0], pos[1], :, :, piece.columns()]
+                    out[0] = windows[0, layer, 0]
+                    both = windows[:3, layer, 1].astype(F32) + windows[1:, layer, 0].astype(F32)
+                    out[1:4] = both.astype(BF16)
+                    out[4] = windows[3, layer, 1]
             self.gather2.start()
+            self.gather2.start_rest()
 
         def forward2(self):
             self.gather2.forward()
@@ -373,6 +391,9 @@
             self.gather2.finish()
             self.gather1.start()
 
+        def rest1(self):
+            self.gather1.start_rest()
+
         def forward1(self):
             self.gather1.forward()
 
@@ -380,8 +401,6 @@
             self.gather1.finish()
 
     flows = [Flow(p, b) for p, b in zip(PIECES, bufs, strict=True)]
-    groups = [flows[3 * c : 3 * c + 3] for c in range(CHUNKS)]
-
     for f in flows:
         f.load()
     state_loads = []
@@ -391,41 +410,47 @@
         state_loads[k].append(load(own, w_in[k]))
     pl.semaphore_wait(barrier, 6)
 
-    def do(c, *names):
-        for name in names:
-            for f in groups[c]:
-                getattr(f, name)()
-
-    do(0, "far1", "near1")
-    for k in range(3):
-        for copy in state_loads[k]:
-            copy.wait()
-    for k in range(2):
-        for win, data in ((m_win[k], m_in[k]), (v_win[k], v_in[k])):
-            win[...] = jnp.zeros_like(win)
-            for layer in (0, 1):
-                for r in range(10):
-                    win[layer, pl.ds(2 * pos[2] + r, 1), :] = data[r, pl.ds(layer, 1), :]
-    do(0, "relay1")
-    do(1, "far1")
-    do(0, "sum1")
-    do(1, "near1", "relay1")
-    do(0, "relay2", "sum2", "relay3", "step", "forward3", "merge", "forward2")
-    do(1, "sum1")
-    do(0, "out1")
-    do(1, "relay2", "sum2")
-    do(0, "forward1")
-    do(1, "relay3", "step", "forward3", "merge", "forward2", "out1", "forward1")
-
-    for k in range(2):
-        for win, out in ((m_win[k], new_m[k]), (v_win[k], new_v[k])):
-            for layer in (0, 1):
-                for r in range(10):
-                    out[r, pl.ds(layer, 1), :] = win[layer, pl.ds(2 * pos[2] + r, 1), :]
-    do(0, "done")
-    do(1, "done")
-    for copy in sent:
-        copy.wait_send()
+    def state_windows():
+        for k in range(3):
+            for copy in state_loads[k]:
+                copy.wait()
+        for k in range(2):
+            for win in (m_win[k], v_win[k]):
+                win[...] = jnp.zeros_like(win)
+
+        def row(r, c):
+            tile, at_row = lax.div(2 * pos[2] + r, 8), pl.ds(lax.rem(2 * pos[2] + r, 8), 1)
+            for k in range(2):
+                for win, data in ((m_win[k], m_in[k]), (v_win[k], v_in[k])):
+                    for layer in (0, 1):
+                        win[layer, tile, at_row, :] = data[r, pl.ds(layer, 1), :]
+            return c
+
+        lax.fori_loop(0, 10, row, 0)
+
+    stage = [0] * len(flows)
+    placed = False
+    for letter in ORDER:
+        i = ord(letter) - ord("a")
+        if stage[i] == 2 and not placed:
+            state_windows()
+            placed = True
+        getattr(flows[i], STAGES[stage[i]])()
+        stage[i] += 1
+
+    def row_out(r, c):
+        tile, at_row = lax.div(2 * pos[2] + r, 8), pl.ds(lax.rem(2 * pos[2] + r, 8), 1)
+        for k in range(2):
+            for win, out in ((m_win[k], new_m[k]), (v_win[k], new_v[k])):
+                for layer in (0, 1):
+                    out[r, pl.ds(layer, 1), :] = win[layer, tile, at_row, :]
+        return c
+
+    lax.fori_loop(0, 10, row_out, 0)
+    for f in flows:
+        f.done()
+    for kind in range(4):
+        wait_sent(kind)
 
 
 def solution(mesh):
@@ -443,9 +468,9 @@
         outs = [(s, BF16) for s in shapes] + [(s, F32) for s in state_shapes] * 2
         scratch = [pltpu.VMEM(s, F32) for s in state_shapes] * 2
         scratch += [pltpu.VMEM((2, 2, 8, 2048), BF16)] * 2 + [pltpu.VMEM((2, 4, 8, 640), BF16)]
-        scratch += [pltpu.VMEM((2, 16, 2048), F32)] * 4
+        scratch += [pltpu.VMEM((2, 2, 8, 2048), F32)] * 4
         scratch += [pltpu.VMEM(s, d) for p in PIECES for s, d in p.scratch()]
-        scratch += [pltpu.SemaphoreType.DMA((COPIES,)), pltpu.SemaphoreType.DMA((COPIES,)), pltpu.SemaphoreType.DMA((LOADS,))]
+        scratch += [pltpu.SemaphoreType.DMA((n,)) for n in (*COPIES, *COPIES, LOADS)]
         new = pl.pallas_call(
             kernel,
             name="step",
@@ -456,6 +481,24 @@
             compiler_params=pltpu.CompilerParams(collective_id=0, has_side_effects=True, vmem_limit_bytes=46 * 2**20),
         )(*terms, *weights, *m, *v)
 
+        def put(*refs):
+            sems = refs[18]
+            copies = [pltpu.make_async_copy(refs[i], refs[9 + i], sems.at[i]) for i in range(9)]
+            for copy in copies:
+                copy.start()
+            for copy in copies:
+                copy.wait()
+
+        new = pl.pallas_call(
+            put,
+            name="put",
+            out_shape=[jax.ShapeDtypeStruct(s, d) for s, d in outs],
+            in_specs=[pl.BlockSpec(memory_space=pltpu.VMEM)] * 9,
+            out_specs=[pl.BlockSpec(memory_space=pl.ANY)] * 9,
+            scratch_shapes=[pltpu.SemaphoreType.DMA((9,))],
+            compiler_params=pltpu.CompilerParams(vmem_limit_bytes=2**20),
+        )(*(pltpu.with_memory_space_constraint(x, pltpu.VMEM) for x in new))
+
         def state_out(x):
             return x.transpose(1, 0, 2) if x.shape[0] == 10 else x.reshape(2, 32, 640)
 

time: 166 us -> 147 us (0.89)
  local copies, waits for them, and re-layouts: 11.1 us -> 0 us
  Pallas kernels: 154 us -> 146 us
    pallas_call x1, Pallas kernels: 154 us -> 140 us  [step(): pl.pallas_call(kernel, name='step', out_shape=[pltpu.VMEM(s, d) for s, d...]
    unnamed x9 -> x0, local copies, waits for them, and re-layouts: 11.1 us -> none
    pallas_call x0 -> x1, Pallas kernels: none -> 5.88 us  [step(): pl.pallas_call(put, name='put', out_shape=[jax.ShapeDtypeStruct(s, d) for...]
where the time goes in v2:
time: 147 us
  Pallas kernels  146 us (99%)
    pallas_call x1, Pallas kernels, step(): pl.pallas_call(kernel, name='step', out_shape=[pltpu.VMEM(s, d) for s, d...  140 us
    pallas_call x1, Pallas kernels, step(): pl.pallas_call(put, name='put', out_shape=[jax.ShapeDtypeStruct(s, d) for...  5.88 us

profile of v2, /device:TPU:0, one launch (start us, length us, event | category | flops | bytes accessed | tf_op | source)
XLA Modules:
  0.0 147.0 jit_solution(5135266740532967817)
XLA Ops:
  0.6 140.5 %step.1 = (bf16[2,4,4,5,8,2048]{5,4,3,2,1,0:T(8,128)(2,1)S(1)}, bf16[2,4,4,5,8,2048]{5,4,3,2,1,0:T(8,128)(2,1)S(1)}, bf16[2,4,4,4,4,8,640]{6,5,4,3,2,1,0:T(8,128...) custom-call(bf16[2,4,4,5,8,2048]{5,4,3,2,1,0:T(8,128)(2,1)} %bitcast, ...), custom_call_target="tpu_custom_call" | custom-call | tf_op jit(solution)/shard_map/step/pallas_call | solution.py:474
  141.1 5.9 %put.1 = (bf16[2,4,4,5,8,2048]{5,4,3,2,1,0:T(8,128)(2,1)}, bf16[2,4,4,5,8,2048]{5,4,3,2,1,0:T(8,128)(2,1)}, bf16[2,4,4,4,4,8,640]{6,5,4,3,2,1,0:T(8,128)(2,1)}, ...) custom-call(bf16[2,4,4,5,8,2048]{5,4,3,2,1,0:T(8,128)(2,1)S(1)} %get, ...), custom_call_target="tpu_custom_call" | custom-call | tf_op jit(solution)/shard_map/put/pallas_call | solution.py:492

commit v3 on v2

--- a/solution.py
+++ b/solution.py
@@ -10,9 +10,9 @@
     *("forward3", "merge", "forward2", "out1", "rest1", "forward1"),
 )
 ORDER = (
-    "abcabcabcdefeabcfefddabcihfieadgibcehhfagdlcgeibalklehbafgdc"
-    "jihkfkgcjlebjaidhfebdhekdgchldjfgahbilgehdkjgcaifgdbljiefhjg"
-    "kcjkcicbbjaaklfhgijkfleefkjddilkihggiljhkljkljkl"
+    "abcabcabcdefeabcfefddabcihfieadgibcehhfagdlcgeibalklehbafgdc",
+    "jihkfkgcjlebjaidhfebdhekdgchldjfgahbilgehdkjgcaifgdbljiefhjg",
+    "kcjkcicbbjaaklfhgijkfleefkjddilkihggiljhkljkljkl",
 )
 
 MESH = pl.DeviceIdType.MESH
@@ -89,8 +89,8 @@
 
 
 PIECES = [Piece(w, c) for c in range(CHUNKS) for w in range(3)]
-COPIES = [12 * n for n in (3 * CHUNKS, 3 * CHUNKS, 2 * CHUNKS, CHUNKS)]
-LOADS = 4 * len(PIECES) + 9
+MOVES = 6 * len(PIECES)
+LOADS = 2 * len(PIECES) + 9
 
 
 def add_into(lead, terms, outs):
@@ -126,8 +126,7 @@
     m_in, v_in, w_in = take(3), take(3), take(3)
     m_win, v_win = take(2), take(2)
     bufs = [take(len(p.scratch())) for p in PIECES]
-    send_sems, recv_sems = take(4), take(4)
-    (load_sem,) = take(1)
+    send_sem, recv_sem, load_sem = take(3)
 
     me = lax.axis_index("dp")
     pos = (lax.div(me, 16), lax.rem(lax.div(me, 4), 4), lax.rem(me, 4))
@@ -146,107 +145,89 @@
     for other in (*plus, *minus):
         pl.semaphore_signal(barrier, inc=1, device_id={"dp": other}, device_id_type=MESH)
 
-    sent, loads = [[], [], [], []], []
-
-    def remote(src, dst, axis, forward, kind):
-        i = len(sent[kind])
-        copy = pltpu.make_async_remote_copy(
-            src_ref=src,
-            dst_ref=dst,
-            send_sem=send_sems[kind].at[i],
-            recv_sem=recv_sems[kind].at[i],
-            device_id={"dp": (plus if forward else minus)[axis]},
-            device_id_type=MESH,
-        )
-        sent[kind].append((src, dst))
-        copy.start()
-        return copy
-
-    def wait_sent(kind):
-        src, dst = sent[kind][0]
-
-        def one(i, c):
+    def wait(sem, like):
+        pltpu.make_async_copy(like, like, sem).wait()
+
+    def load(src, dst, sem):
+        pltpu.make_async_copy(src, dst, sem).start()
+
+    class Move:
+        made = 0
+
+        def __init__(self, axis, recv):
+            self.axis, self.recv, self.index = axis, recv, Move.made
+            Move.made += 1
+
+        def remote(self, src, dst, forward, first):
             pltpu.make_async_remote_copy(
                 src_ref=src,
                 dst_ref=dst,
-                send_sem=send_sems[kind].at[i],
-                recv_sem=recv_sems[kind].at[i],
-                device_id={"dp": plus[0]},
+                send_sem=send_sem.at[self.index],
+                recv_sem=recv_sem.at[2 * self.index + (0 if first else 1)],
+                device_id={"dp": (plus if forward else minus)[self.axis]},
                 device_id_type=MESH,
-            ).wait_send()
-            return c
-
-        lax.fori_loop(0, len(sent[kind]), one, 0)
-
-    def load(src, dst):
-        copy = pltpu.make_async_copy(src, dst, load_sem.at[len(loads)])
-        loads.append(copy)
-        copy.start()
-        return copy
-
-    class Scatter:
-        def __init__(self, kind, axis, recv, far, near, lead, relay_term):
-            self.kind, self.axis, self.recv, self.far, self.near = kind, axis, recv, far, near
-            self.lead, self.relay_term = lead, relay_term
-            self.got = {}
+            ).start()
+
+        def wait_first(self):
+            wait(recv_sem.at[2 * self.index], self.recv.at[0])
+
+        def wait_rest(self):
+            wait(recv_sem.at[2 * self.index + 1], self.recv.at[pl.ds(1, 2)])
+
+        def wait_sent(self):
+            wait(send_sem.at[self.index], self.recv)
+
+    class Scatter(Move):
+        def __init__(self, axis, recv, far, near, lead, relay_term):
+            super().__init__(axis, recv)
+            self.far, self.near, self.lead, self.relay_term = far, near, lead, relay_term
 
         def send_far(self):
             for layer in (0, 1):
-                self.got["far", layer] = remote(self.far(layer), self.recv.at[0, layer], self.axis, layer == 0, self.kind)
+                self.remote(self.far(layer), self.recv.at[0, layer], layer == 0, True)
 
         def send_near(self):
             for layer in (1, 0):
-                self.got["near", layer] = remote(self.near(layer), self.recv.at[1, layer], self.axis, layer == 1, self.kind)
+                self.remote(self.near(layer), self.recv.at[1, layer], layer == 1, False)
 
         def relay(self):
-            for layer in (0, 1):
-                self.got["far", layer].wait_recv()
+            self.wait_first()
+            for layer in (0, 1):
                 here = self.recv.at[0, layer]
                 add_into(self.lead, (here, self.relay_term(layer)), (here,))
-                self.got["relay", layer] = remote(here, self.recv.at[2, layer], self.axis, layer == 0, self.kind)
-
-        def wait(self, layer):
-            self.got["near", layer].wait_recv()
-            self.got["relay", layer].wait_recv()
-
-    class Gather:
-        def __init__(self, kind, axis, block):
-            self.kind, self.axis, self.block = kind, axis, block
-            self.got = {}
-
-        def send(self, layer, p, forward, key):
+                self.remote(here, self.recv.at[2, layer], layer == 0, False)
+
+    class Gather(Move):
+        def __init__(self, axis, recv, block):
+            super().__init__(axis, recv)
+            self.block = block
+
+        def send(self, layer, p, forward, first):
             ref = self.block(layer, p)
-            self.got[key] = remote(ref, ref, self.axis, forward, self.kind)
+            self.remote(ref, ref, forward, first)
 
         def start(self):
             mine = pos[self.axis]
-            self.send(0, mine, True, "from minus 0")
-            self.send(1, mine, False, "from plus 1")
+            self.send(0, mine, True, True)
+            self.send(1, mine, False, True)
 
         def start_rest(self):
             mine = pos[self.axis]
-            self.send(1, mine, True, "from minus 1")
-            self.send(0, mine, False, "from plus 0")
+            self.send(1, mine, True, False)
+            self.send(0, mine, False, False)
 
         def forward(self):
-            self.got["from minus 0"].wait_recv()
-            self.send(0, at(self.axis, 3), True, "far 0")
-            self.got["from plus 1"].wait_recv()
-            self.send(1, at(self.axis, 1), False, "far 1")
-
-        def finish(self):
-            for key in ("from minus 1", "from plus 0", "far 0", "far 1"):
-                self.got[key].wait_recv()
+            self.wait_first()
+            self.send(0, at(self.axis, 3), True, False)
+            self.send(1, at(self.axis, 1), False, False)
 
     class Flow:
         def __init__(self, piece, buf):
             self.piece, self.buf = piece, buf
             a1, a2, a3 = piece.axes
-            last = 2 if piece.weight < 2 else 3
             g = grads[piece.weight]
             own1, recv1, sum1, send1, recv2, sum2, send2, recv3 = buf[:8]
             self.scatter1 = Scatter(
-                0,
                 a1,
                 recv1,
                 lambda layer: piece.first(g, layer, at(a1, 2)),
@@ -255,7 +236,6 @@
                 lambda layer: own1.at[layer, 1],
             )
             self.scatter2 = Scatter(
-                1,
                 a2,
                 recv2,
                 lambda layer: send1.at[layer, 0],
@@ -264,7 +244,6 @@
                 lambda layer: sum1.at[layer, 1],
             )
             self.scatter3 = Scatter(
-                last,
                 a3,
                 recv3,
                 lambda layer: piece.third(send2.at[layer], at(a3, 2)),
@@ -275,20 +254,22 @@
             w = new_w[piece.weight]
             if piece.weight < 2:
                 windows = buf[8]
-                self.gather3 = Gather(last, a3, lambda layer, p: windows.at[p, layer])
+                self.gather3 = Gather(a3, recv3, lambda layer, p: windows.at[p, layer])
             else:
-                self.gather3 = Gather(last, a3, lambda layer, p: piece.out3(w, layer, p, pos))
-            self.gather2 = Gather(1, a2, lambda layer, p: piece.out2(w, layer, p, pos))
-            self.gather1 = Gather(0, a1, lambda layer, p: piece.first(w, layer, p))
-
-        def load(self):
+                self.gather3 = Gather(a3, recv3, lambda layer, p: piece.out3(w, layer, p, pos))
+            self.gather2 = Gather(a2, recv2, lambda layer, p: piece.out2(w, layer, p, pos))
+            self.gather1 = Gather(a1, recv1, lambda layer, p: piece.first(w, layer, p))
+
+            self.moves = (self.scatter1, self.scatter2, self.scatter3, self.gather3, self.gather2, self.gather1)
+
+        def load(self, index):
             piece, own1 = self.piece, self.buf[0]
             a1, g = piece.axes[0], grads[piece.weight]
-            self.loaded = [[None, None], [None, None]]
+            self.loaded = [load_sem.at[2 * index], load_sem.at[2 * index + 1]]
             for which in (1, 0):
                 for layer in (0, 1):
                     p = at(a1, (3 if layer else 1) if which else 0)
-                    self.loaded[layer][which] = load(piece.first(g, layer, p), own1.at[layer, which])
+                    load(piece.first(g, layer, p), own1.at[layer, which], self.loaded[which])
 
         def far1(self):
             self.scatter1.send_far()
@@ -297,17 +278,15 @@
             self.scatter1.send_near()
 
         def relay1(self):
-            for layer in (0, 1):
-                self.loaded[layer][1].wait()
+            wait(self.loaded[1], self.buf[0].at[:, 1])
             self.scatter1.relay()
 
         def sum1(self):
             piece = self.piece
             own1, recv1, sum1, send1 = self.buf[:4]
             a2 = piece.axes[1]
-            for layer in (0, 1):
-                self.loaded[layer][0].wait()
-                self.scatter1.wait(layer)
+            wait(self.loaded[0], own1.at[:, 0])
+            self.scatter1.wait_rest()
 
             def reduce(layer, d, out):
                 p = at(a2, d)
@@ -330,8 +309,8 @@
 
         def sum2(self):
             sum1, _, recv2, sum2, send2 = self.buf[2:7]
-            for layer in (0, 1):
-                self.scatter2.wait(layer)
+            self.scatter2.wait_rest()
+            for layer in (0, 1):
                 terms = (sum1.at[layer, 0], recv2.at[1, layer], recv2.at[2, layer])
                 add_into(self.piece.lead2, terms, (sum2.at[layer], send2.at[layer]))
             self.scatter3.send_far()
@@ -344,8 +323,8 @@
             piece = self.piece
             sum2, recv3 = self.buf[5], self.buf[7]
             a3, k = piece.axes[2], piece.weight
-            for layer in (0, 1):
-                self.scatter3.wait(layer)
+            self.scatter3.wait_rest()
+            for layer in (0, 1):
                 terms = (piece.third(sum2.at[layer], pos[a3]), recv3.at[1, layer], recv3.at[2, layer])
                 g = terms[0][...] + terms[1][...].astype(F32) + terms[2][...].astype(F32)
                 g = g.astype(BF16).astype(F32)
@@ -372,7 +351,7 @@
 
         def merge(self):
             piece = self.piece
-            self.gather3.finish()
+            self.gather3.wait_rest()
             if piece.weight < 2:
                 windows, k = self.buf[8], piece.weight
                 for layer in (0, 1):
@@ -388,7 +367,7 @@
             self.gather2.forward()
 
         def out1(self):
-            self.gather2.finish()
+            self.gather2.wait_rest()
             self.gather1.start()
 
         def rest1(self):
@@ -398,22 +377,22 @@
             self.gather1.forward()
 
         def done(self):
-            self.gather1.finish()
+            self.gather1.wait_rest()
 
     flows = [Flow(p, b) for p, b in zip(PIECES, bufs, strict=True)]
-    for f in flows:
-        f.load()
-    state_loads = []
+    for i, f in enumerate(flows):
+        f.load(i)
+    state = []
     for k in range(3):
-        state_loads.append([load(ms[k], m_in[k]), load(vs[k], v_in[k])])
         own = weights[k].at[:, pos[0], pos[1], pl.ds(pos[2], 2)] if k < 2 else weights[k].at[:, pos[0], pos[1], pos[2]]
-        state_loads[k].append(load(own, w_in[k]))
+        state += [(ms[k], m_in[k]), (vs[k], v_in[k]), (own, w_in[k])]
+    for i, (src, dst) in enumerate(state):
+        load(src, dst, load_sem.at[2 * len(flows) + i])
     pl.semaphore_wait(barrier, 6)
 
     def state_windows():
-        for k in range(3):
-            for copy in state_loads[k]:
-                copy.wait()
+        for i, (_, dst) in enumerate(state):
+            wait(load_sem.at[2 * len(flows) + i], dst)
         for k in range(2):
             for win in (m_win[k], v_win[k]):
                 win[...] = jnp.zeros_like(win)
@@ -430,7 +409,7 @@
 
     stage = [0] * len(flows)
     placed = False
-    for letter in ORDER:
+    for letter in "".join(ORDER):
         i = ord(letter) - ord("a")
         if stage[i] == 2 and not placed:
             state_windows()
@@ -449,8 +428,9 @@
     lax.fori_loop(0, 10, row_out, 0)
     for f in flows:
         f.done()
-    for kind in range(4):
-        wait_sent(kind)
+    for f in flows:
+        for move in f.moves:
+            move.wait_sent()
 
 
 def solution(mesh):
@@ -470,7 +450,7 @@
         scratch += [pltpu.VMEM((2, 2, 8, 2048), BF16)] * 2 + [pltpu.VMEM((2, 4, 8, 640), BF16)]
         scratch += [pltpu.VMEM((2, 2, 8, 2048), F32)] * 4
         scratch += [pltpu.VMEM(s, d) for p in PIECES for s, d in p.scratch()]
-        scratch += [pltpu.SemaphoreType.DMA((n,)) for n in (*COPIES, *COPIES, LOADS)]
+        scratch += [pltpu.SemaphoreType.DMA((n,)) for n in (MOVES, 2 * MOVES, LOADS)]
         new = pl.pallas_call(
             kernel,
             name="step",

time: 147 us -> 138 us (0.939)
  Pallas kernels: 146 us -> 138 us
    pallas_call x1, Pallas kernels: 140 us -> 132 us  [step(): pl.pallas_call(kernel, name='step', out_shape=[pltpu.VMEM(s, d) for s, d...]
where the time goes in v3:
time: 138 us
  Pallas kernels  138 us (100%)
    pallas_call x1, Pallas kernels, step(): pl.pallas_call(kernel, name='step', out_shape=[pltpu.VMEM(s, d) for s, d...  132 us
    pallas_call x1, Pallas kernels, step(): pl.pallas_call(put, name='put', out_shape=[jax.ShapeDtypeStruct(s, d) for...  5.88 us

profile of v3, /device:TPU:0, one launch (start us, length us, event | category | flops | bytes accessed | tf_op | source)
XLA Modules:
  0.0 138.2 jit_solution(13303124943802322846)
XLA Ops:
  0.6 131.7 %step.1 = (bf16[2,4,4,5,8,2048]{5,4,3,2,1,0:T(8,128)(2,1)S(1)}, bf16[2,4,4,5,8,2048]{5,4,3,2,1,0:T(8,128)(2,1)S(1)}, bf16[2,4,4,4,4,8,640]{6,5,4,3,2,1,0:T(8,128...) custom-call(bf16[2,4,4,5,8,2048]{5,4,3,2,1,0:T(8,128)(2,1)} %bitcast, ...), custom_call_target="tpu_custom_call" | custom-call | tf_op jit(solution)/shard_map/step/pallas_call | solution.py:454
  132.4 5.9 %put.1 = (bf16[2,4,4,5,8,2048]{5,4,3,2,1,0:T(8,128)(2,1)}, bf16[2,4,4,5,8,2048]{5,4,3,2,1,0:T(8,128)(2,1)}, bf16[2,4,4,4,4,8,640]{6,5,4,3,2,1,0:T(8,128)(2,1)}, ...) custom-call(bf16[2,4,4,5,8,2048]{5,4,3,2,1,0:T(8,128)(2,1)S(1)} %get, ...), custom_call_target="tpu_custom_call" | custom-call | tf_op jit(solution)/shard_map/put/pallas_call | solution.py:472

commit v4 on v3

--- a/solution.py
+++ b/solution.py
@@ -10,24 +10,26 @@
     *("forward3", "merge", "forward2", "out1", "rest1", "forward1"),
 )
 ORDER = (
-    "abcabcabcdefeabcfefddabcihfieadgibcehhfagdlcgeibalklehbafgdc",
-    "jihkfkgcjlebjaidhfebdhekdgchldjfgahbilgehdkjgcaifgdbljiefhjg",
-    "kcjkcicbbjaaklfhgijkfleefkjddilkihggiljhkljkljkl",
+    "cadafcedbabbceffiebcadhegabgcdihaffjgcdheibkcladfhbgelfhckjg",
+    "dkjcfabilgdhkjafbdgielckjbgahileahgecjkfdlbighkacliebaiklhdb",
+    "bifgljkejchdeikcfahghjkliigjlldjikkhgjflfeekldjj",
 )
 
 MESH = pl.DeviceIdType.MESH
 F32, BF16 = jnp.float32, jnp.bfloat16
 CHUNKS = 4
 COLS = 2048 // CHUNKS
+EARLY = 1
 TILES = 4 // CHUNKS
 
 
 class Piece:
     def __init__(self, weight, chunk):
         self.weight, self.chunk = weight, chunk
+        self.early = weight < 2 and chunk == EARLY
         if weight < 2:
-            self.axes = ((0, 1, 2), (1, 0, 2))[weight]
-            self.lead1, self.lead2, self.lead3 = (4, 5), (5,), (2,)
+            self.axes = ((0, 2, 1), (1, 2, 0))[weight] if self.early else ((0, 1, 2), (1, 0, 2))[weight]
+            self.lead1, self.lead2, self.lead3 = (4, 5), (4, 2) if self.early else (5,), (2,)
             self.cols = COLS
         else:
             self.axes = ((2, 0, 1), (2, 1, 0))[chunk % 2]
@@ -50,7 +52,7 @@
             (self.shape(three, 3, 2), BF16),
         ]
         if self.weight < 2:
-            shapes.append((self.shape(three, 4, 2), BF16))
+            shapes.append((self.shape(two if self.early else three, 4, 2), BF16))
         return shapes
 
     def columns(self):
@@ -64,12 +66,14 @@
         return ref.at[layer, :, :, p, pl.ds(self.chunk * TILES, TILES)]
 
     def second(self, block, p):
+        if self.early:
+            return block.at[:, pl.ds(p, 2)]
         if self.weight == 2 and self.axes[1] == 1:
             return block.at[:, p]
         return block.at[p]
 
     def third(self, block, p):
-        return block.at[pl.ds(p, 2)] if self.weight < 2 else block.at[p]
+        return block.at[p] if self.weight == 2 or self.early else block.at[pl.ds(p, 2)]
 
     def out2(self, ref, layer, p, pos):
         if self.weight == 0:
@@ -89,8 +93,8 @@
 
 
 PIECES = [Piece(w, c) for c in range(CHUNKS) for w in range(3)]
-MOVES = 6 * len(PIECES)
-LOADS = 2 * len(PIECES) + 9
+MOVES = 3 * len(PIECES)
+LOADS = 2 * CHUNKS + 4
 
 
 def add_into(lead, terms, outs):
@@ -101,7 +105,7 @@
         for o in outs:
             o[index] = total.astype(o.dtype)
 
-    if len(lead) + (lead[-1] == 5) > 2:
+    if len(lead) > 2 or lead == (4, 5):
         lax.fori_loop(0, lead[0], lambda i, c: (body(i), c)[1], 0)
     else:
         body(...)
@@ -148,38 +152,40 @@
     def wait(sem, like):
         pltpu.make_async_copy(like, like, sem).wait()
 
+    loaded = set()
+
     def load(src, dst, sem):
         pltpu.make_async_copy(src, dst, sem).start()
 
     class Move:
-        made = 0
-
-        def __init__(self, axis, recv):
-            self.axis, self.recv, self.index = axis, recv, Move.made
-            Move.made += 1
+        def __init__(self, index, axis, recv):
+            self.axis, self.recv, self.sems = axis, recv, (3 * index, 3 * index + self.rest)
+            self.sent = send_sem.at[index]
 
         def remote(self, src, dst, forward, first):
             pltpu.make_async_remote_copy(
                 src_ref=src,
                 dst_ref=dst,
-                send_sem=send_sem.at[self.index],
-                recv_sem=recv_sem.at[2 * self.index + (0 if first else 1)],
+                send_sem=self.sent,
+                recv_sem=recv_sem.at[self.sems[0 if first else 1]],
                 device_id={"dp": (plus if forward else minus)[self.axis]},
                 device_id_type=MESH,
             ).start()
 
         def wait_first(self):
-            wait(recv_sem.at[2 * self.index], self.recv.at[0])
+            wait(recv_sem.at[self.sems[0]], self.recv.at[0])
 
         def wait_rest(self):
-            wait(recv_sem.at[2 * self.index + 1], self.recv.at[pl.ds(1, 2)])
+            wait(recv_sem.at[self.sems[1]], self.recv.at[pl.ds(1, 2)])
 
         def wait_sent(self):
-            wait(send_sem.at[self.index], self.recv)
+            wait(self.sent, self.recv)
 
     class Scatter(Move):
-        def __init__(self, axis, recv, far, near, lead, relay_term):
-            super().__init__(axis, recv)
+        rest = 1
+
+        def __init__(self, index, axis, recv, far, near, lead, relay_term):
+            super().__init__(index, axis, recv)
             self.far, self.near, self.lead, self.relay_term = far, near, lead, relay_term
 
         def send_far(self):
@@ -198,15 +204,18 @@
                 self.remote(here, self.recv.at[2, layer], layer == 0, False)
 
     class Gather(Move):
-        def __init__(self, axis, recv, block):
-            super().__init__(axis, recv)
-            self.block = block
+        rest = 2
+
+        def __init__(self, scatter, index, block):
+            super().__init__(index, scatter.axis, scatter.recv)
+            self.scatter, self.block = scatter, block
 
         def send(self, layer, p, forward, first):
             ref = self.block(layer, p)
             self.remote(ref, ref, forward, first)
 
         def start(self):
+            self.scatter.wait_sent()
             mine = pos[self.axis]
             self.send(0, mine, True, True)
             self.send(1, mine, False, True)
@@ -222,12 +231,13 @@
             self.send(1, at(self.axis, 1), False, False)
 
     class Flow:
-        def __init__(self, piece, buf):
+        def __init__(self, index, piece, buf):
             self.piece, self.buf = piece, buf
             a1, a2, a3 = piece.axes
             g = grads[piece.weight]
             own1, recv1, sum1, send1, recv2, sum2, send2, recv3 = buf[:8]
             self.scatter1 = Scatter(
+                3 * index,
                 a1,
                 recv1,
                 lambda layer: piece.first(g, layer, at(a1, 2)),
@@ -236,6 +246,7 @@
                 lambda layer: own1.at[layer, 1],
             )
             self.scatter2 = Scatter(
+                3 * index + 1,
                 a2,
                 recv2,
                 lambda layer: send1.at[layer, 0],
@@ -244,6 +255,7 @@
                 lambda layer: sum1.at[layer, 1],
             )
             self.scatter3 = Scatter(
+                3 * index + 2,
                 a3,
                 recv3,
                 lambda layer: piece.third(send2.at[layer], at(a3, 2)),
@@ -254,22 +266,31 @@
             w = new_w[piece.weight]
             if piece.weight < 2:
                 windows = buf[8]
-                self.gather3 = Gather(a3, recv3, lambda layer, p: windows.at[p, layer])
+                if piece.early:
+                    self.gather3 = Gather(self.scatter3, 3 * index + 2, lambda layer, p: windows.at[pos[2], layer, p])
+                else:
+                    self.gather3 = Gather(self.scatter3, 3 * index + 2, lambda layer, p: windows.at[p, layer])
             else:
-                self.gather3 = Gather(a3, recv3, lambda layer, p: piece.out3(w, layer, p, pos))
-            self.gather2 = Gather(a2, recv2, lambda layer, p: piece.out2(w, layer, p, pos))
-            self.gather1 = Gather(a1, recv1, lambda layer, p: piece.first(w, layer, p))
-
-            self.moves = (self.scatter1, self.scatter2, self.scatter3, self.gather3, self.gather2, self.gather1)
-
-        def load(self, index):
+                self.gather3 = Gather(self.scatter3, 3 * index + 2, lambda layer, p: piece.out3(w, layer, p, pos))
+            if piece.early:
+                self.gather2 = Gather(self.scatter2, 3 * index + 1, lambda layer, p: windows.at[p, layer])
+            else:
+                self.gather2 = Gather(self.scatter2, 3 * index + 1, lambda layer, p: piece.out2(w, layer, p, pos))
+            self.gather1 = Gather(self.scatter1, 3 * index, lambda layer, p: piece.first(w, layer, p))
+
+        def load(self):
             piece, own1 = self.piece, self.buf[0]
             a1, g = piece.axes[0], grads[piece.weight]
-            self.loaded = [load_sem.at[2 * index], load_sem.at[2 * index + 1]]
             for which in (1, 0):
                 for layer in (0, 1):
                     p = at(a1, (3 if layer else 1) if which else 0)
-                    load(piece.first(g, layer, p), own1.at[layer, which], self.loaded[which])
+                    load(piece.first(g, layer, p), own1.at[layer, which], load_sem.at[2 * piece.chunk + which])
+
+        def wait_load(self, which):
+            i = 2 * self.piece.chunk + which
+            if i not in loaded:
+                loaded.add(i)
+                wait(load_sem.at[i], self.buf[1])
 
         def far1(self):
             self.scatter1.send_far()
@@ -278,14 +299,14 @@
             self.scatter1.send_near()
 
         def relay1(self):
-            wait(self.loaded[1], self.buf[0].at[:, 1])
+            self.wait_load(1)
             self.scatter1.relay()
 
         def sum1(self):
             piece = self.piece
             own1, recv1, sum1, send1 = self.buf[:4]
             a2 = piece.axes[1]
-            wait(self.loaded[0], own1.at[:, 0])
+            self.wait_load(0)
             self.scatter1.wait_rest()
 
             def reduce(layer, d, out):
@@ -336,7 +357,8 @@
                     v_win[k][layer, :, :, cols] = v
                     row = lax.broadcasted_iota(jnp.int32, w.shape, 1) + 8 * lax.broadcasted_iota(jnp.int32, w.shape, 0)
                     mine = (row >= 2 * pos[2]) & (row < 2 * pos[2] + 10)
-                    self.buf[8][pos[2], layer] = jnp.where(mine, w, 0.0).astype(BF16)
+                    windows = self.gather3.block(layer, pos[a3])
+                    windows[...] = jnp.where(mine, w, 0.0).astype(BF16)
                 else:
                     t = pl.ds(piece.chunk * TILES, TILES)
                     w, m, v = adamw(w_in[k][layer, t].astype(F32), m_in[k][layer, t], v_in[k][layer, t], g)
@@ -350,24 +372,29 @@
             self.gather3.forward()
 
         def merge(self):
-            piece = self.piece
             self.gather3.wait_rest()
-            if piece.weight < 2:
-                windows, k = self.buf[8], piece.weight
-                for layer in (0, 1):
-                    out = new_w[k].at[layer, pos[0], pos[1], :, :, piece.columns()]
-                    out[0] = windows[0, layer, 0]
-                    both = windows[:3, layer, 1].astype(F32) + windows[1:, layer, 0].astype(F32)
-                    out[1:4] = both.astype(BF16)
-                    out[4] = windows[3, layer, 1]
+            if self.piece.weight < 2 and not self.piece.early:
+                self.join(lambda t: (pos[self.piece.axes[1]], t))
             self.gather2.start()
             self.gather2.start_rest()
 
+        def join(self, tile):
+            piece, windows = self.piece, self.buf[8]
+            for layer in (0, 1):
+                out = piece.first(new_w[piece.weight], layer, pos[piece.axes[0]])
+                part = [windows.at[z, layer, :, j] if piece.early else windows.at[z, layer, j] for z in range(4) for j in (0, 1)]
+                out[tile(0)] = part[0][...]
+                for t in (1, 2, 3):
+                    out[tile(t)] = (part[2 * t - 1][...].astype(F32) + part[2 * t][...].astype(F32)).astype(BF16)
+                out[tile(4)] = part[7][...]
+
         def forward2(self):
             self.gather2.forward()
 
         def out1(self):
             self.gather2.wait_rest()
+            if self.piece.early:
+                self.join(lambda t: (slice(None), t))
             self.gather1.start()
 
         def rest1(self):
@@ -379,20 +406,21 @@
         def done(self):
             self.gather1.wait_rest()
 
-    flows = [Flow(p, b) for p, b in zip(PIECES, bufs, strict=True)]
-    for i, f in enumerate(flows):
-        f.load(i)
-    state = []
+    flows = [Flow(i, p, b) for i, (p, b) in enumerate(zip(PIECES, bufs, strict=True))]
+    for f in flows:
+        f.load()
+    state_sem = 2 * CHUNKS
     for k in range(3):
         own = weights[k].at[:, pos[0], pos[1], pl.ds(pos[2], 2)] if k < 2 else weights[k].at[:, pos[0], pos[1], pos[2]]
-        state += [(ms[k], m_in[k]), (vs[k], v_in[k]), (own, w_in[k])]
-    for i, (src, dst) in enumerate(state):
-        load(src, dst, load_sem.at[2 * len(flows) + i])
+        load(own, w_in[k], load_sem.at[state_sem + 1 + k])
+        load(ms[k], m_in[k], load_sem.at[state_sem])
+        load(vs[k], v_in[k], load_sem.at[state_sem])
     pl.semaphore_wait(barrier, 6)
 
     def state_windows():
-        for i, (_, dst) in enumerate(state):
-            wait(load_sem.at[2 * len(flows) + i], dst)
+        wait(load_sem.at[state_sem], bufs[0][1])
+        for k in range(3):
+            wait(load_sem.at[state_sem + 1 + k], w_in[k])
         for k in range(2):
             for win in (m_win[k], v_win[k]):
                 win[...] = jnp.zeros_like(win)
@@ -429,8 +457,8 @@
     for f in flows:
         f.done()
     for f in flows:
-        for move in f.moves:
-            move.wait_sent()
+        for gather in (f.gather3, f.gather2, f.gather1):
+            gather.wait_sent()
 
 
 def solution(mesh):
@@ -450,7 +478,7 @@
         scratch += [pltpu.VMEM((2, 2, 8, 2048), BF16)] * 2 + [pltpu.VMEM((2, 4, 8, 640), BF16)]
         scratch += [pltpu.VMEM((2, 2, 8, 2048), F32)] * 4
         scratch += [pltpu.VMEM(s, d) for p in PIECES for s, d in p.scratch()]
-        scratch += [pltpu.SemaphoreType.DMA((n,)) for n in (MOVES, 2 * MOVES, LOADS)]
+        scratch += [pltpu.SemaphoreType.DMA((n,)) for n in (MOVES, 3 * MOVES, LOADS)]
         new = pl.pallas_call(
             kernel,
             name="step",

time: 138 us -> 136 us (0.986)
  Pallas kernels: 138 us -> 135 us
    pallas_call x1, Pallas kernels: 132 us -> 130 us  [step(): pl.pallas_call(kernel, name='step', out_shape=[pltpu.VMEM(s, d) for s, d...]
where the time goes in v4:
time: 136 us
  Pallas kernels  135 us (99%)
    pallas_call x1, Pallas kernels, step(): pl.pallas_call(kernel, name='step', out_shape=[pltpu.VMEM(s, d) for s, d...  130 us
    pallas_call x1, Pallas kernels, step(): pl.pallas_call(put, name='put', out_shape=[jax.ShapeDtypeStruct(s, d) for...  5.88 us

profile of v4, /device:TPU:0, one launch (start us, length us, event | category | flops | bytes accessed | tf_op | source)
XLA Modules:
  0.0 136.1 jit_solution(963465179039671555)
XLA Ops:
  0.6 129.6 %step.1 = (bf16[2,4,4,5,8,2048]{5,4,3,2,1,0:T(8,128)(2,1)S(1)}, bf16[2,4,4,5,8,2048]{5,4,3,2,1,0:T(8,128)(2,1)S(1)}, bf16[2,4,4,4,4,8,640]{6,5,4,3,2,1,0:T(8,128...) custom-call(bf16[2,4,4,5,8,2048]{5,4,3,2,1,0:T(8,128)(2,1)} %bitcast, ...), custom_call_target="tpu_custom_call" | custom-call | tf_op jit(solution)/shard_map/step/pallas_call | solution.py:482
  130.2 5.9 %put.1 = (bf16[2,4,4,5,8,2048]{5,4,3,2,1,0:T(8,128)(2,1)}, bf16[2,4,4,5,8,2048]{5,4,3,2,1,0:T(8,128)(2,1)}, bf16[2,4,4,4,4,8,640]{6,5,4,3,2,1,0:T(8,128)(2,1)}, ...) custom-call(bf16[2,4,4,5,8,2048]{5,4,3,2,1,0:T(8,128)(2,1)S(1)} %get, ...), custom_call_target="tpu_custom_call" | custom-call | tf_op jit(solution)/shard_map/put/pallas_call | solution.py:500

commit v5 on v4

--- a/solution.py
+++ b/solution.py
@@ -93,8 +93,9 @@
 
 
 PIECES = [Piece(w, c) for c in range(CHUNKS) for w in range(3)]
-MOVES = 3 * len(PIECES)
-LOADS = 2 * CHUNKS + 4
+LOADS = 2 * CHUNKS + 5
+
+RECEIVES = ((0, 1), (2, 3), (4, 5), (4, 3), (2, 1), (0, 6))
 
 
 def add_into(lead, terms, outs):
@@ -129,6 +130,7 @@
     new_w, new_m, new_v = take(3), take(3), take(3)
     m_in, v_in, w_in = take(3), take(3), take(3)
     m_win, v_win = take(2), take(2)
+    ahead = take(3)
     bufs = [take(len(p.scratch())) for p in PIECES]
     send_sem, recv_sem, load_sem = take(3)
 
@@ -158,9 +160,10 @@
         pltpu.make_async_copy(src, dst, sem).start()
 
     class Move:
-        def __init__(self, index, axis, recv):
-            self.axis, self.recv, self.sems = axis, recv, (3 * index, 3 * index + self.rest)
-            self.sent = send_sem.at[index]
+        def __init__(self, index, stage, axis, recv):
+            self.axis, self.recv = axis, recv
+            self.sent = send_sem.at[2 * index + stage % 2]
+            self.sems = [7 * index + i for i in RECEIVES[stage]]
 
         def remote(self, src, dst, forward, first):
             pltpu.make_async_remote_copy(
@@ -182,10 +185,8 @@
             wait(self.sent, self.recv)
 
     class Scatter(Move):
-        rest = 1
-
-        def __init__(self, index, axis, recv, far, near, lead, relay_term):
-            super().__init__(index, axis, recv)
+        def __init__(self, index, stage, axis, recv, far, near, lead, relay_term):
+            super().__init__(index, stage, axis, recv)
             self.far, self.near, self.lead, self.relay_term = far, near, lead, relay_term
 
         def send_far(self):
@@ -204,18 +205,15 @@
                 self.remote(here, self.recv.at[2, layer], layer == 0, False)
 
     class Gather(Move):
-        rest = 2
-
-        def __init__(self, scatter, index, block):
-            super().__init__(index, scatter.axis, scatter.recv)
-            self.scatter, self.block = scatter, block
+        def __init__(self, index, stage, scatter, block):
+            super().__init__(index, stage, scatter.axis, scatter.recv)
+            self.block = block
 
         def send(self, layer, p, forward, first):
             ref = self.block(layer, p)
             self.remote(ref, ref, forward, first)
 
         def start(self):
-            self.scatter.wait_sent()
             mine = pos[self.axis]
             self.send(0, mine, True, True)
             self.send(1, mine, False, True)
@@ -237,16 +235,18 @@
             g = grads[piece.weight]
             own1, recv1, sum1, send1, recv2, sum2, send2, recv3 = buf[:8]
             self.scatter1 = Scatter(
-                3 * index,
+                index,
+                0,
                 a1,
                 recv1,
-                lambda layer: piece.first(g, layer, at(a1, 2)),
+                lambda layer: piece.first(g, layer, at(a1, 2)) if piece.chunk else ahead[piece.weight].at[layer],
                 lambda layer: piece.first(g, layer, at(a1, 1 if layer else 3)),
                 piece.lead1,
                 lambda layer: own1.at[layer, 1],
             )
             self.scatter2 = Scatter(
-                3 * index + 1,
+                index,
+                1,
                 a2,
                 recv2,
                 lambda layer: send1.at[layer, 0],
@@ -255,7 +255,8 @@
                 lambda layer: sum1.at[layer, 1],
             )
             self.scatter3 = Scatter(
-                3 * index + 2,
+                index,
+                2,
                 a3,
                 recv3,
                 lambda layer: piece.third(send2.at[layer], at(a3, 2)),
@@ -267,16 +268,16 @@
             if piece.weight < 2:
                 windows = buf[8]
                 if piece.early:
-                    self.gather3 = Gather(self.scatter3, 3 * index + 2, lambda layer, p: windows.at[pos[2], layer, p])
+                    self.gather3 = Gather(index, 3, self.scatter3, lambda layer, p: windows.at[pos[2], layer, p])
                 else:
-                    self.gather3 = Gather(self.scatter3, 3 * index + 2, lambda layer, p: windows.at[p, layer])
+                    self.gather3 = Gather(index, 3, self.scatter3, lambda layer, p: windows.at[p, layer])
             else:
-                self.gather3 = Gather(self.scatter3, 3 * index + 2, lambda layer, p: piece.out3(w, layer, p, pos))
+                self.gather3 = Gather(index, 3, self.scatter3, lambda layer, p: piece.out3(w, layer, p, pos))
             if piece.early:
-                self.gather2 = Gather(self.scatter2, 3 * index + 1, lambda layer, p: windows.at[p, layer])
+                self.gather2 = Gather(index, 4, self.scatter2, lambda layer, p: windows.at[p, layer])
             else:
-                self.gather2 = Gather(self.scatter2, 3 * index + 1, lambda layer, p: piece.out2(w, layer, p, pos))
-            self.gather1 = Gather(self.scatter1, 3 * index, lambda layer, p: piece.first(w, layer, p))
+                self.gather2 = Gather(index, 4, self.scatter2, lambda layer, p: piece.out2(w, layer, p, pos))
+            self.gather1 = Gather(index, 5, self.scatter1, lambda layer, p: piece.first(w, layer, p))
 
         def load(self):
             piece, own1 = self.piece, self.buf[0]
@@ -334,6 +335,7 @@
             for layer in (0, 1):
                 terms = (sum1.at[layer, 0], recv2.at[1, layer], recv2.at[2, layer])
                 add_into(self.piece.lead2, terms, (sum2.at[layer], send2.at[layer]))
+            self.scatter1.wait_sent()
             self.scatter3.send_far()
             self.scatter3.send_near()
 
@@ -365,6 +367,7 @@
                     new_m[k][layer, t] = m
                     new_v[k][layer, t] = v
                     new_w[k][layer, pos[0], pos[1], pos[2], t] = w.astype(BF16)
+            self.scatter2.wait_sent()
             self.gather3.start()
             self.gather3.start_rest()
 
@@ -375,6 +378,7 @@
             self.gather3.wait_rest()
             if self.piece.weight < 2 and not self.piece.early:
                 self.join(lambda t: (pos[self.piece.axes[1]], t))
+            self.scatter3.wait_sent()
             self.gather2.start()
             self.gather2.start_rest()
 
@@ -395,6 +399,7 @@
             self.gather2.wait_rest()
             if self.piece.early:
                 self.join(lambda t: (slice(None), t))
+            self.gather3.wait_sent()
             self.gather1.start()
 
         def rest1(self):
@@ -407,6 +412,9 @@
             self.gather1.wait_rest()
 
     flows = [Flow(i, p, b) for i, (p, b) in enumerate(zip(PIECES, bufs, strict=True))]
+    for f, dst in zip(flows, ahead, strict=False):
+        for layer in (0, 1):
+            load(f.piece.first(grads[f.piece.weight], layer, at(f.piece.axes[0], 2)), dst.at[layer], load_sem.at[LOADS - 1])
     for f in flows:
         f.load()
     state_sem = 2 * CHUNKS
@@ -415,6 +423,7 @@
         load(own, w_in[k], load_sem.at[state_sem + 1 + k])
         load(ms[k], m_in[k], load_sem.at[state_sem])
         load(vs[k], v_in[k], load_sem.at[state_sem])
+    wait(load_sem.at[LOADS - 1], bufs[0][1])
     pl.semaphore_wait(barrier, 6)
 
     def state_windows():
@@ -457,7 +466,7 @@
     for f in flows:
         f.done()
     for f in flows:
-        for gather in (f.gather3, f.gather2, f.gather1):
+        for gather in (f.gather2, f.gather1):
             gather.wait_sent()
 
 
@@ -477,8 +486,9 @@
         scratch = [pltpu.VMEM(s, F32) for s in state_shapes] * 2
         scratch += [pltpu.VMEM((2, 2, 8, 2048), BF16)] * 2 + [pltpu.VMEM((2, 4, 8, 640), BF16)]
         scratch += [pltpu.VMEM((2, 2, 8, 2048), F32)] * 4
+        scratch += [pltpu.VMEM(p.shape(p.lead1, 2), BF16) for p in PIECES[:3]]
         scratch += [pltpu.VMEM(s, d) for p in PIECES for s, d in p.scratch()]
-        scratch += [pltpu.SemaphoreType.DMA((n,)) for n in (MOVES, 3 * MOVES, LOADS)]
+        scratch += [pltpu.SemaphoreType.DMA((n,)) for n in (2 * len(PIECES), 7 * len(PIECES), LOADS)]
         new = pl.pallas_call(
             kernel,
             name="step",

time: 136 us -> 135 us (level)
  no operation moved by 1% of the time
where the time goes in v5:
time: 135 us
  Pallas kernels  134 us (99%)
    pallas_call x1, Pallas kernels, step(): pl.pallas_call(kernel, name='step', out_shape=[pltpu.VMEM(s, d) for s, d...  128 us
    pallas_call x1, Pallas kernels, step(): pl.pallas_call(put, name='put', out_shape=[jax.ShapeDtypeStruct(s, d) for...  5.88 us

profile of v5, /device:TPU:0, one launch (start us, length us, event | category | flops | bytes accessed | tf_op | source)
XLA Modules:
  0.0 134.8 jit_solution(824959383758796197)
XLA Ops:
  0.6 128.3 %step.1 = (bf16[2,4,4,5,8,2048]{5,4,3,2,1,0:T(8,128)(2,1)S(1)}, bf16[2,4,4,5,8,2048]{5,4,3,2,1,0:T(8,128)(2,1)S(1)}, bf16[2,4,4,4,4,8,640]{6,5,4,3,2,1,0:T(8,128...) custom-call(bf16[2,4,4,5,8,2048]{5,4,3,2,1,0:T(8,128)(2,1)} %bitcast, ...), custom_call_target="tpu_custom_call" | custom-call | tf_op jit(solution)/shard_map/step/pallas_call | solution.py:492
  128.9 5.9 %put.1 = (bf16[2,4,4,5,8,2048]{5,4,3,2,1,0:T(8,128)(2,1)}, bf16[2,4,4,5,8,2048]{5,4,3,2,1,0:T(8,128)(2,1)}, bf16[2,4,4,4,4,8,640]{6,5,4,3,2,1,0:T(8,128)(2,1)}, ...) custom-call(bf16[2,4,4,5,8,2048]{5,4,3,2,1,0:T(8,128)(2,1)S(1)} %get, ...), custom_call_target="tpu_custom_call" | custom-call | tf_op jit(solution)/shard_map/put/pallas_call | solution.py:510

commit v6 on v5

--- a/solution.py
+++ b/solution.py
@@ -10,9 +10,9 @@
     *("forward3", "merge", "forward2", "out1", "rest1", "forward1"),
 )
 ORDER = (
-    "cadafcedbabbceffiebcadhegabgcdihaffjgcdheibkcladfhbgelfhckjg",
-    "dkjcfabilgdhkjafbdgielckjbgahileahgecjkfdlbighkacliebaiklhdb",
-    "bifgljkejchdeikcfahghjkliigjlldjikkhgjflfeekldjj",
+    "abebheddcfacgfadcfiibeabjfhabgekdciehgcjbadfkklbchjgalfedabh",
+    "lkcgdfjebchigdakfjelbghcadkfeijblghafkjcidlbhgkalijcfabekdaj",
+    "ihgblckecichgljeeikffgidgjdlhillljfkdkghhijelkij",
 )
 
 MESH = pl.DeviceIdType.MESH

time: 135 us -> 133 us (0.985)
    pallas_call x1, Pallas kernels: 128 us -> 127 us  [step(): pl.pallas_call(kernel, name='step', out_shape=[pltpu.VMEM(s, d) for s, d...]
where the time goes in v6:
time: 133 us
  Pallas kernels  133 us (100%)
    pallas_call x1, Pallas kernels, step(): pl.pallas_call(kernel, name='step', out_shape=[pltpu.VMEM(s, d) for s, d...  127 us
    pallas_call x1, Pallas kernels, step(): pl.pallas_call(put, name='put', out_shape=[jax.ShapeDtypeStruct(s, d) for...  5.88 us

profile of v6, /device:TPU:0, one launch (start us, length us, event | category | flops | bytes accessed | tf_op | source)
XLA Modules:
  0.0 133.4 jit_solution(8610137904845308610)
XLA Ops:
  0.6 126.8 %step.1 = (bf16[2,4,4,5,8,2048]{5,4,3,2,1,0:T(8,128)(2,1)S(1)}, bf16[2,4,4,5,8,2048]{5,4,3,2,1,0:T(8,128)(2,1)S(1)}, bf16[2,4,4,4,4,8,640]{6,5,4,3,2,1,0:T(8,128...) custom-call(bf16[2,4,4,5,8,2048]{5,4,3,2,1,0:T(8,128)(2,1)} %bitcast, ...), custom_call_target="tpu_custom_call" | custom-call | tf_op jit(solution)/shard_map/step/pallas_call | solution.py:492
  127.5 5.9 %put.1 = (bf16[2,4,4,5,8,2048]{5,4,3,2,1,0:T(8,128)(2,1)}, bf16[2,4,4,5,8,2048]{5,4,3,2,1,0:T(8,128)(2,1)}, bf16[2,4,4,4,4,8,640]{6,5,4,3,2,1,0:T(8,128)(2,1)}, ...) custom-call(bf16[2,4,4,5,8,2048]{5,4,3,2,1,0:T(8,128)(2,1)S(1)} %get, ...), custom_call_target="tpu_custom_call" | custom-call | tf_op jit(solution)/shard_map/put/pallas_call | solution.py:510

commit v7 on v6

--- a/solution.py
+++ b/solution.py
@@ -93,7 +93,7 @@
 
 
 PIECES = [Piece(w, c) for c in range(CHUNKS) for w in range(3)]
-LOADS = 2 * CHUNKS + 5
+LOADS = CHUNKS + 5
 
 RECEIVES = ((0, 1), (2, 3), (4, 5), (4, 3), (2, 1), (0, 6))
 
@@ -285,13 +285,13 @@
             for which in (1, 0):
                 for layer in (0, 1):
                     p = at(a1, (3 if layer else 1) if which else 0)
-                    load(piece.first(g, layer, p), own1.at[layer, which], load_sem.at[2 * piece.chunk + which])
-
-        def wait_load(self, which):
-            i = 2 * self.piece.chunk + which
+                    load(piece.first(g, layer, p), own1.at[layer, which], load_sem.at[piece.chunk])
+
+        def wait_load(self):
+            i = self.piece.chunk
             if i not in loaded:
                 loaded.add(i)
-                wait(load_sem.at[i], self.buf[1])
+                wait(load_sem.at[i], grads[0].at[:, :3, :2])
 
         def far1(self):
             self.scatter1.send_far()
@@ -300,14 +300,13 @@
             self.scatter1.send_near()
 
         def relay1(self):
-            self.wait_load(1)
+            self.wait_load()
             self.scatter1.relay()
 
         def sum1(self):
             piece = self.piece
             own1, recv1, sum1, send1 = self.buf[:4]
             a2 = piece.axes[1]
-            self.wait_load(0)
             self.scatter1.wait_rest()
 
             def reduce(layer, d, out):
@@ -417,7 +416,7 @@
             load(f.piece.first(grads[f.piece.weight], layer, at(f.piece.axes[0], 2)), dst.at[layer], load_sem.at[LOADS - 1])
     for f in flows:
         f.load()
-    state_sem = 2 * CHUNKS
+    state_sem = CHUNKS
     for k in range(3):
         own = weights[k].at[:, pos[0], pos[1], pl.ds(pos[2], 2)] if k < 2 else weights[k].at[:, pos[0], pos[1], pos[2]]
         load(own, w_in[k], load_sem.at[state_sem + 1 + k])
@@ -463,11 +462,11 @@
         return c
 
     lax.fori_loop(0, 10, row_out, 0)
-    for f in flows:
-        f.done()
-    for f in flows:
-        for gather in (f.gather2, f.gather1):
-            gather.wait_sent()
+    whole_order = "".join(ORDER)
+    for i in sorted(range(len(flows)), key=lambda i: whole_order.rindex(chr(ord("a") + i))):
+        flows[i].done()
+        flows[i].gather2.wait_sent()
+        flows[i].gather1.wait_sent()
 
 
 def solution(mesh):
@@ -501,11 +500,13 @@
 
         def put(*refs):
             sems = refs[18]
-            copies = [pltpu.make_async_copy(refs[i], refs[9 + i], sems.at[i]) for i in range(9)]
+            copies = [pltpu.make_async_copy(refs[i], refs[9 + i], sems.at[min(i, 3)]) for i in range(9)]
             for copy in copies:
                 copy.start()
-            for copy in copies:
+            for copy in copies[:3]:
                 copy.wait()
+            moments = refs[0].at[:, 0, :3]
+            pltpu.make_async_copy(moments, moments, sems.at[3]).wait()
 
         new = pl.pallas_call(
             put,
@@ -513,7 +514,7 @@
             out_shape=[jax.ShapeDtypeStruct(s, d) for s, d in outs],
             in_specs=[pl.BlockSpec(memory_space=pltpu.VMEM)] * 9,
             out_specs=[pl.BlockSpec(memory_space=pl.ANY)] * 9,
-            scratch_shapes=[pltpu.SemaphoreType.DMA((9,))],
+            scratch_shapes=[pltpu.SemaphoreType.DMA((4,))],
             compiler_params=pltpu.CompilerParams(vmem_limit_bytes=2**20),
         )(*(pltpu.with_memory_space_constraint(x, pltpu.VMEM) for x in new))
 

time: 133 us -> 133 us (level)
  no operation moved by 1% of the time
where the time goes in v7:
time: 133 us
  Pallas kernels  133 us (100%)
    pallas_call x1, Pallas kernels, step(): pl.pallas_call(kernel, name='step', out_shape=[pltpu.VMEM(s, d) for s, d...  127 us
    pallas_call x1, Pallas kernels, step(): pl.pallas_call(put, name='put', out_shape=[jax.ShapeDtypeStruct(s, d) for...  5.83 us

profile of v7, /device:TPU:0, one launch (start us, length us, event | category | flops | bytes accessed | tf_op | source)
XLA Modules:
  0.0 133.2 jit_solution(5075201248082854189)
XLA Ops:
  0.6 126.8 %step.1 = (bf16[2,4,4,5,8,2048]{5,4,3,2,1,0:T(8,128)(2,1)S(1)}, bf16[2,4,4,5,8,2048]{5,4,3,2,1,0:T(8,128)(2,1)S(1)}, bf16[2,4,4,4,4,8,640]{6,5,4,3,2,1,0:T(8,128...) custom-call(bf16[2,4,4,5,8,2048]{5,4,3,2,1,0:T(8,128)(2,1)} %bitcast, ...), custom_call_target="tpu_custom_call" | custom-call | tf_op jit(solution)/shard_map/step/pallas_call | solution.py:491
  127.4 5.8 %put.1 = (bf16[2,4,4,5,8,2048]{5,4,3,2,1,0:T(8,128)(2,1)}, bf16[2,4,4,5,8,2048]{5,4,3,2,1,0:T(8,128)(2,1)}, bf16[2,4,4,4,4,8,640]{6,5,4,3,2,1,0:T(8,128)(2,1)}, ...) custom-call(bf16[2,4,4,5,8,2048]{5,4,3,2,1,0:T(8,128)(2,1)S(1)} %get, ...), custom_call_target="tpu_custom_call" | custom-call | tf_op jit(solution)/shard_map/put/pallas_call | solution.py:511
